TPU v7x, 32 devices: a whole 2x2x4 slice. The times are simulated.
32 devices in a mesh: group: 4 (over z), dom: 8 (over y, x, core).
Axes of the slice: x: 2, y: 2, z: 4, core: 2. Of those that a mesh axis runs over, the one named last changes fastest.
Arguments:
- features: bfloat16 [16384, 128], P(('group', 'dom')), may hold values from -6 to 6
- cotangent: bfloat16 [16384, 128], P(('group', 'dom')), may hold values from -6 to 6
- fine_send: int32 [256, 16], P(('group', 'dom')), may hold values from 0 to 512, as said below
- fine_rim: int32 [64, 128], P(('group', 'dom')), may hold values from 0 to 511
- fine_src: int32 [131072], P(('group', 'dom')), may hold values from 0 to 895, as said below
- fine_dst: int32 [131072], P(('group', 'dom')), may hold values from 0 to 511
- fine_pool: int32 [16384], P(('group', 'dom')), may hold values from 0 to 255, as said below
- coarse_send: int32 [256, 4], P(('group', 'dom')), may hold values from 0 to 32, as said below
- coarse_src: int32 [8192], P(('group', 'dom')), may hold values from 0 to 63, as said below
- coarse_dst: int32 [8192], P(('group', 'dom')), may hold values from 0 to 31
- coarse_pool: int32 [1024], P(('group', 'dom')), may hold values from 0 to 511
- w_send: bfloat16 [128, 128], replicated, may hold values from -0.5 to 0.5
- w_recv: bfloat16 [128, 128], replicated, may hold values from -0.5 to 0.5
- w_node: bfloat16 [128, 128], replicated, may hold values from -0.5 to 0.5
- v_send: bfloat16 [128, 128], replicated, may hold values from -0.5 to 0.5
- v_recv: bfloat16 [128, 128], replicated, may hold values from -0.5 to 0.5
- v_node: bfloat16 [128, 128], replicated, may hold values from -0.5 to 0.5
- w_top: bfloat16 [128, 128], replicated, may hold values from -0.5 to 0.5
Outputs:
- flow: bfloat16 [16384, 128], P(('group', 'dom'))
- grad_features: float32 [16384, 128], P(('group', 'dom'))
- grad_send: float32 [128, 128], replicated
Inputs may be any that keep to these rules, and one draw needn't show every extreme that they name: `fine_send`: each device holds 8 rows of 16: row p lists own node rows for the device with dom index p of its group; the value 512 marks an empty slot, live slots come first, and three rows of every device are full. `fine_rim`: each device holds two rows: the first go to the previous group's device of the same dom index, the second to the next group's. `fine_src`: index into the device's extended rows: its 512 nodes, 128 rows from its group in dom order, 128 rows from the previous group, 128 from the next. `fine_pool`: coarse node numbered within the node's group. `coarse_send`: as fine_send with 4 slots a row and 32 marking an empty slot. `coarse_src`: index into the device's coarse rows, then 8 * 4 rows from its group in dom order.
All inputs are finite; a program needn't handle non-finite values.
Results may differ from a plain program's by a relative error of at most 0.025.
Values may be sent and summed in bfloat16 or wider, within the bound.
No kernel may reach another device: no remote copies, remote signals or barrier semaphores. Data moves between devices by JAX's collectives and lax.ppermute only.
A program may use at most 64 MiB of HBM per device.

v0:
```python
import jax
import jax.numpy as jnp
from jax import lax
from jax.sharding import PartitionSpec as P

NCC = 512


def with_halo(block, sides, width):
    for axis, dim in sides:
        count = lax.axis_size(axis)
        forward = [(i, i + 1) for i in range(count - 1)]
        backward = [(target, source) for source, target in forward]
        low = lax.ppermute(
            lax.slice_in_dim(block, block.shape[dim] - width, None, axis=dim), axis, forward
        )
        high = lax.ppermute(lax.slice_in_dim(block, 0, width, axis=dim), axis, backward)
        block = jnp.concatenate([low, block, high], axis=dim)
    return block


def silu_slope(values):
    sigma = jax.nn.sigmoid(values)
    return sigma * (1.0 + values * (1.0 - sigma))


def edge_forward(extended, own_rows, sources, targets, w_send, w_recv, w_node):
    preact = jnp.dot(extended[sources], w_send, preferred_element_type=jnp.float32)
    preact = preact + jnp.dot(own_rows[targets], w_recv, preferred_element_type=jnp.float32)
    message = jax.nn.silu(preact).astype(jnp.bfloat16)
    summed = jax.ops.segment_sum(
        message.astype(jnp.float32), targets, num_segments=own_rows.shape[0]
    ).astype(jnp.bfloat16)
    updated = (
        own_rows.astype(jnp.float32) + jnp.dot(summed, w_node, preferred_element_type=jnp.float32)
    ).astype(jnp.bfloat16)
    return (updated, preact)


def edge_backward(grad_out, extended, own_rows, preact, sources, targets, w_send, w_recv, w_node):
    rounded = grad_out.astype(jnp.bfloat16)
    grad_sum = jnp.dot(rounded, w_node.T, preferred_element_type=jnp.float32)
    grad_pre = (grad_sum[targets] * silu_slope(preact)).astype(jnp.bfloat16)
    grad_ext = jax.ops.segment_sum(
        jnp.dot(grad_pre, w_send.T, preferred_element_type=jnp.float32),
        sources,
        num_segments=extended.shape[0],
    )
    own_count = own_rows.shape[0]
    grad_own = grad_out + jax.ops.segment_sum(
        jnp.dot(grad_pre, w_recv.T, preferred_element_type=jnp.float32),
        targets,
        num_segments=own_count,
    )
    grad_own = grad_own + grad_ext[:own_count]
    grad_weight = lax.dot_general(
        extended[sources], grad_pre, (((0,), (0,)), ((), ())), preferred_element_type=jnp.float32
    )
    return (grad_own, grad_ext[own_count:], grad_weight)


def top_forward(pooled, w_top):
    slope_in = jnp.dot(pooled.astype(jnp.bfloat16), w_top, preferred_element_type=jnp.float32)
    return ((pooled + jax.nn.silu(slope_in)).astype(jnp.bfloat16), slope_in)


def top_backward(grad_top, slope_in, w_top):
    inner = (grad_top * silu_slope(slope_in)).astype(jnp.bfloat16)
    return grad_top + jnp.dot(inner, w_top.T, preferred_element_type=jnp.float32)


def add_rows(grads, index, values):
    padded = jnp.concatenate([grads, jnp.zeros((1, grads.shape[1]), jnp.float32)], axis=0)
    return padded.at[index].add(values)[:-1]


def local(
    features,
    cotangent,
    fine_send,
    fine_rim,
    fine_src,
    fine_dst,
    fine_pool,
    coarse_send,
    coarse_src,
    coarse_dst,
    coarse_pool,
    w_send,
    w_recv,
    w_node,
    v_send,
    v_recv,
    v_node,
    w_top,
):
    width = features.shape[1]
    dom_count = lax.axis_size("dom")
    coarse_count = coarse_pool.shape[0]
    group_coarse = coarse_count * dom_count
    slot_rows = fine_send.shape[1]
    coarse_slots = coarse_send.shape[1]
    rim_count = fine_rim.shape[1]
    padded = jnp.concatenate([features, jnp.zeros((1, width), jnp.bfloat16)], axis=0)
    incoming = lax.all_to_all(
        padded[fine_send], "dom", split_axis=0, concat_axis=0, tiled=True
    ).reshape(-1, width)
    rim_rows = with_halo(features[fine_rim], (("group", 0),), 1)
    extended = jnp.concatenate([features, incoming, rim_rows[0], rim_rows[3]], axis=0)
    updated, preact = edge_forward(extended, features, fine_src, fine_dst, w_send, w_recv, w_node)
    partial_value = jax.ops.segment_sum(
        updated.astype(jnp.float32), fine_pool, num_segments=group_coarse
    )
    grad_flow = cotangent.astype(jnp.float32)
    grad_partial = jax.ops.segment_sum(grad_flow, fine_pool, num_segments=group_coarse)
    owned = lax.psum_scatter(partial_value, "dom", scatter_dimension=0, tiled=True)
    grad_coarse = lax.psum_scatter(grad_partial, "dom", scatter_dimension=0, tiled=True)
    coarse_in = (0.25 * owned).astype(jnp.bfloat16)
    cpadded = jnp.concatenate([coarse_in, jnp.zeros((1, width), jnp.bfloat16)], axis=0)
    cincoming = lax.all_to_all(
        cpadded[coarse_send], "dom", split_axis=0, concat_axis=0, tiled=True
    ).reshape(-1, width)
    cextended = jnp.concatenate([coarse_in, cincoming], axis=0)
    coarse_mid, cpreact = edge_forward(
        cextended, coarse_in, coarse_src, coarse_dst, v_send, v_recv, v_node
    )
    top_partial = jax.ops.segment_sum(coarse_mid.astype(jnp.float32), coarse_pool, num_segments=NCC)
    grad_top_partial = jax.ops.segment_sum(grad_coarse, coarse_pool, num_segments=NCC)
    top_total = lax.psum(top_partial, ("group", "dom"))
    grad_top = lax.psum(grad_top_partial, ("group", "dom"))
    pooled = 0.125 * top_total
    top_out, slope_in = top_forward(pooled, w_top)
    coarse_out = (coarse_mid.astype(jnp.float32) + top_out[coarse_pool].astype(jnp.float32)).astype(
        jnp.bfloat16
    )
    coarse_table = lax.all_gather(coarse_out, "dom", axis=0, tiled=True)
    flow = (updated.astype(jnp.float32) + coarse_table[fine_pool].astype(jnp.float32)).astype(
        jnp.bfloat16
    )
    grad_pool = top_backward(grad_top, slope_in, w_top)
    grad_cmid = grad_coarse + 0.125 * grad_pool[coarse_pool]
    c_own, c_halo, c_weight = edge_backward(
        grad_cmid, cextended, coarse_in, cpreact, coarse_src, coarse_dst, v_send, v_recv, v_node
    )
    creturned = lax.all_to_all(
        c_halo.reshape(dom_count, coarse_slots, width),
        "dom",
        split_axis=0,
        concat_axis=0,
        tiled=True,
    )
    grad_cin = add_rows(c_own, coarse_send.reshape(-1), creturned.reshape(-1, width))
    grad_table = lax.all_gather(grad_cin, "dom", axis=0, tiled=True)
    grad_fmid = grad_flow + 0.25 * grad_table[fine_pool]
    f_own, f_halo, f_weight = edge_backward(
        grad_fmid, extended, features, preact, fine_src, fine_dst, w_send, w_recv, w_node
    )
    split = dom_count * slot_rows
    returned = lax.all_to_all(
        f_halo[:split].reshape(dom_count, slot_rows, width),
        "dom",
        split_axis=0,
        concat_axis=0,
        tiled=True,
    )
    grad_x = add_rows(f_own, fine_send.reshape(-1), returned.reshape(-1, width))
    rim_grads = jnp.stack([f_halo[split : split + rim_count], f_halo[split + rim_count :]], axis=0)
    rim_back = with_halo(rim_grads, (("group", 0),), 1)
    rim_values = jnp.concatenate([rim_back[0], rim_back[3]], axis=0)
    grad_x = add_rows(grad_x, fine_rim.reshape(-1), rim_values)
    grad_send = lax.psum(f_weight, ("group", "dom"))
    return (flow, grad_x, grad_send)


def solution(mesh):
    placed = (
        P(("group", "dom"), None),
        P(("group", "dom"), None),
        P(("group", "dom"), None),
        P(("group", "dom"), None),
        P(("group", "dom")),
        P(("group", "dom")),
        P(("group", "dom")),
        P(("group", "dom"), None),
        P(("group", "dom")),
        P(("group", "dom")),
        P(("group", "dom")),
        P(),
        P(),
        P(),
        P(),
        P(),
        P(),
        P(),
    )
    return jax.shard_map(
        local,
        mesh=mesh,
        in_specs=placed,
        out_specs=(P(("group", "dom"), None), P(("group", "dom"), None), P()),
        check_vma=False,
    )
```

profile of v0, /device:TPU:0, one launch (start us, length us, event | category | flops | bytes accessed | tf_op | source)
XLA Modules:
  0.0 538.0 jit_solution(17636104793602975725)
XLA Ops:
  10.9 5.6 %collective-permute-start = (bf16[1,128,128]{2,1,0:T(8,128)(2,1)S(1)}, bf16[1,128,128]{2,1,0:T(8,128)(2,1)S(1)}, u32[]{:S(2)}, u32[]{:S(2)}) collective-permute-start(bf16[1,128,128]{2,1,0:T(8,128)(2,1)S(1)} %get-tuple-element.8), channel_id=1, source_target_pairs={{0,8},{8,16},{16,24},{1,9},{9,17},{17,25},{2,10},{10,18},{18,26},{... | collective-permute-start | bytes 98312 | tf_op jit(solution)/shard_map/ppermute | solution.py:14
  19.5 4.2 all-to-all-start
  24.4 12.1 %gather_fusion.3 = bf16[4096,128]{1,0:T(8,128)(2,1)S(1)} fusion(bf16[512,128]{1,0:T(8,128)(2,1)S(1)} %copy-done.1, s32[4096]{0:T(1024)S(1)} %fusion.37), kind=kCustom, calls=%fused_computation.3 | custom fusion | bytes 2113536 | tf_op jit(solution)/shard_map/gather | solution.py:29
  38.4 12.1 %gather_fusion.2 = bf16[4096,128]{1,0:T(8,128)(2,1)S(1)} fusion(bf16[896,128]{1,0:T(8,128)(2,1)S(1)} %pad_maximum_fusion, s32[4096]{0:T(1024)S(1)} %fusion.36), kind=kCustom, calls=%fused_computation.2 | custom fusion | bytes 2113536 | tf_op jit(solution)/shard_map/gather | solution.py:28
  52.6 23.8 %scatter_custom_fusion = f32[512,128]{1,0:T(8,128)} fusion(s32[4096]{0:T(1024)} %param.23, f32[4096,128]{1,0:T(8,128)S(1)} %convolution_add_fusion, f32[]{:T(128)} %constant.20.clone.1, f32[]{:T(128)} %constant.14.clone.1), kind=kCustom, calls=%fused_computation.28 | custom fusion | flops 3670016 | bytes 2360320 | tf_op jit(solution)/shard_map/scatter-add | solution.py:31
  78.2 3.2 scatter_custom_fusion.1
  81.6 3.0 scatter_custom_fusion.4
  91.5 24.4 %reduce-scatter.3.cloned.1.call-done = f32[32,128]{1,0:T(8,128)} async-done(((f32[256,128]{1,0:T(8,128)}), f32[32,128]{1,0:T(8,128)}) %reduce-scatter.3.cloned.1.call-update) | async-done | bytes 16400 | tf_op jit(solution)/shard_map/reduce_scatter | solution.py:116
  117.8 3.3 all-to-all-start.1
  121.8 31.3 %reduce-scatter.5.cloned.1.call-done = f32[32,128]{1,0:T(8,128)} async-done(((f32[256,128]{1,0:T(8,128)}), f32[32,128]{1,0:T(8,128)}) %reduce-scatter.5.cloned.1.call-update) | async-done | bytes 16400 | tf_op jit(solution)/shard_map/reduce_scatter | solution.py:117
  163.2 127.0 %all-reduce.10.cloned.1.call-done = (f32[512,128]{1,0:T(8,128)}, f32[512,128]{1,0:T(8,128)}) async-done(((f32[512,128]{1,0:T(8,128)}, f32[512,128]{1,0:T(8,128)}), (f32[512,128]{1,0:T(8,128)}, f32[512,128]{1,0:T(8,128)})) %all-reduce.10.cloned.1.call-update) | async-done | bytes 524304 | tf_op jit(solution)/shard_map/psum | solution.py:129
  292.8 9.4 %all_gather.6 = bf16[256,128]{1,0:T(8,128)(2,1)S(1)} all-gather(bf16[32,128]{1,0:T(8,128)(2,1)S(1)} %add_convert_fusion.2), channel_id=1, replica_groups=mesh['group'=4,'dom'=8] {'dom'}, dimensions={0}, use_global_device_ids=true | all-gather | bytes 73728 | tf_op jit(solution)/shard_map/all_gather | solution.py:136
  305.3 2.1 convolution_add_fusion.1
  314.9 3.3 all-to-all-start.2
  320.4 2.5 all-to-all-done.2
  323.7 8.2 %all_gather.7 = f32[256,128]{1,0:T(8,128)S(1)} all-gather(f32[32,128]{1,0:T(8,128)S(1)} %slice.78), channel_id=1, replica_groups=mesh['group'=4,'dom'=8] {'dom'}, dimensions={0}, use_global_device_ids=true | all-gather | bytes 147456 | tf_op jit(solution)/shard_map/all_gather | solution.py:153
  334.8 14.2 %gather_fusion.12 = f32[4096,128]{1,0:T(8,128)} fusion(f32[512,128]{1,0:T(8,128)S(1)} %fusion.15, s32[4096]{0:T(1024)S(1)} %fusion.37), kind=kCustom, calls=%fused_computation.12 | custom fusion | bytes 4210688 | tf_op jit(solution)/shard_map/gather | solution.py:43
  349.0 2.4 multiply_convert_fusion
  354.7 22.8 %scatter_custom_fusion.9 = f32[896,128]{1,0:T(8,128)S(1)} fusion(s32[4096]{0:T(1024)} %param.22, f32[4096,128]{1,0:T(8,128)} %fusion.56, f32[]{:T(128)} %constant.14.clone.1), kind=kCustom, calls=%fused_computation.54 | custom fusion | flops 524288 | bytes 459264 | tf_op jit(solution)/shard_map/scatter-add | solution.py:44
  378.1 3.3 all-to-all-start.3
  382.6 22.5 %scatter_fusion.2 = f32[512,128]{1,0:T(8,128)S(1)} fusion(f32[512,128]{1,0:T(8,128)S(1)} %slice_add_fusion, s32[4096]{0:T(1024)S(1)} %copy-done.10, f32[4096,128]{1,0:T(8,128)S(1)} %fusion.57), kind=kCustom, calls=%fused_computation.23 | custom fusion | flops 524288 | bytes 6307840 | tf_op jit(solution)/shard_map/scatter-add | solution.py:50
  406.4 4.5 collective-permute-start.2
  412.8 2.1 scatter_custom_fusion.12
  415.7 114.3 %all-reduce.8.cloned.1.call-done = f32[128,128]{1,0:T(8,128)} async-done(((f32[128,128]{1,0:T(8,128)}), f32[128,128]{1,0:T(8,128)}) %all-reduce.8.cloned.1.call-update) | async-done | bytes 65552 | tf_op jit(solution)/shard_map/psum | solution.py:171
  (133 shorter events, 62.0 us)
Async XLA Ops:
  7.2 43.4 %copy-start = (bf16[128,128]{1,0:T(8,128)(2,1)S(1)}, bf16[128,128]{1,0:T(8,128)(2,1)}, u32[]{:S(2)}) copy-start(bf16[128,128]{1,0:T(8,128)(2,1)} %param.29) | copy-start | bytes 98308
  9.6 28.8 %collective-permute-start.1 = (bf16[1,128,128]{2,1,0:T(8,128)(2,1)S(1)}, bf16[1,128,128]{2,1,0:T(8,128)(2,1)S(1)}, u32[]{:S(2)}, u32[]{:S(2)}) collective-permute-start(bf16[1,128,128]{2,1,0:T(8,128)(2,1)S(1)} %get-tuple-element.9), channel_id=1, source_target_pairs={{8,0},{16,8},{24,16},{9,1},{17,9},{25,17},{10,2},{18,10},{26,18},{... | collective-permute-start | bytes 98312 | tf_op jit(solution)/shard_map/ppermute | solution.py:17
  10.9 27.5 %collective-permute-start = (bf16[1,128,128]{2,1,0:T(8,128)(2,1)S(1)}, bf16[1,128,128]{2,1,0:T(8,128)(2,1)S(1)}, u32[]{:S(2)}, u32[]{:S(2)}) collective-permute-start(bf16[1,128,128]{2,1,0:T(8,128)(2,1)S(1)} %get-tuple-element.8), channel_id=1, source_target_pairs={{0,8},{8,16},{16,24},{1,9},{9,17},{17,25},{2,10},{10,18},{18,26},{... | collective-permute-start | bytes 98312 | tf_op jit(solution)/shard_map/ppermute | solution.py:14
  19.5 18.9 %all-to-all-start = ((bf16[8,16,128]{2,1,0:T(8,128)(2,1)}), bf16[8,16,128]{2,1,0:T(8,128)(2,1)S(1)}, u32[]{:S(2)}, u32[]{:S(2)}) async-start(bf16[8,16,128]{2,1,0:T(8,128)(2,1)} %bitcast), calls=%async_computation | async-start | bytes 65536 | tf_op jit(solution)/shard_map/all_to_all | solution.py:105
  23.7 92.2 %reduce-scatter.3.cloned.1.call-start = ((), (), s32[]{:S(2)}) async-start(), calls=%async_computation.6 | async-start | bytes 147456 | tf_op jit(solution)/shard_map/reduce_scatter | solution.py:116
  52.6 29.0 %copy-start.3 = (bf16[512,128]{1,0:T(8,128)(2,1)S(1)}, bf16[512,128]{1,0:T(8,128)(2,1)}, u32[]{:S(2)}) copy-start(bf16[512,128]{1,0:T(8,128)(2,1)} %param.19) | copy-start | bytes 393220
  76.4 79.9 %copy-start.5 = (bf16[128,128]{1,0:T(8,128)(2,1)S(1)}, bf16[128,128]{1,0:T(8,128)(2,1)}, u32[]{:S(2)}) copy-start(bf16[128,128]{1,0:T(8,128)(2,1)} %param.32) | copy-start | bytes 98308
  76.4 82.6 %copy-start.7 = (bf16[128,128]{1,0:T(8,128)(2,1)S(1)}, bf16[128,128]{1,0:T(8,128)(2,1)}, u32[]{:S(2)}) copy-start(bf16[128,128]{1,0:T(8,128)(2,1)} %param.34) | copy-start | bytes 98308
  81.5 71.5 %reduce-scatter.5.cloned.1.call-start = ((), (), s32[]{:S(2)}) async-start(), calls=%async_computation.7 | async-start | bytes 147456 | tf_op jit(solution)/shard_map/reduce_scatter | solution.py:117
  89.6 65.8 %copy-start.16 = (s32[1024]{0:T(1024)}, s32[1024]{0:T(1024)S(1)}, u32[]{:S(2)}) copy-start(s32[1024]{0:T(1024)S(1)} %pad_clamp_fusion.2) | copy-start | bytes 12292
  117.8 37.7 %all-to-all-start.1 = ((bf16[8,4,128]{2,1,0:T(4,128)(2,1)}), bf16[8,4,128]{2,1,0:T(4,128)(2,1)S(1)}, u32[]{:S(2)}, u32[]{:S(2)}) async-start(bf16[8,4,128]{2,1,0:T(4,128)(2,1)} %bitcast.7), calls=%async_computation.2 | async-start | bytes 16384 | tf_op jit(solution)/shard_map/all_to_all | solution.py:120
  121.2 169.0 %all-reduce.10.cloned.1.call-start = ((), (), s32[]{:S(2)}) async-start(), calls=%async_computation.9 | async-start | bytes 1048576 | tf_op jit(solution)/shard_map/psum | solution.py:129
  311.6 20.4 %copy-start.15 = (s32[1024]{0:T(1024)S(1)}, s32[1024]{0:T(1024)}, u32[]{:S(2)}) copy-start(s32[1024]{0:T(1024)} %pad_clamp_fusion) | copy-start | bytes 12292
  314.9 8.0 %all-to-all-start.2 = ((f32[8,4,128]{2,1,0:T(4,128)}), f32[8,4,128]{2,1,0:T(4,128)S(1)}, u32[]{:S(2)}, u32[]{:S(2)}) async-start(f32[8,4,128]{2,1,0:T(4,128)} %bitcast.10), calls=%async_computation.4 | async-start | bytes 32768 | tf_op jit(solution)/shard_map/all_to_all | solution.py:145
  353.5 28.0 %copy-start.2 = (f32[512,128]{1,0:T(8,128)S(1)}, f32[512,128]{1,0:T(8,128)}, u32[]{:S(2)}) copy-start(f32[512,128]{1,0:T(8,128)} %gather_fusion.11) | copy-start | bytes 786436
  353.6 29.0 %copy-start.10 = (s32[4096]{0:T(1024)S(1)}, s32[4096]{0:T(1024)}, u32[]{:S(2)}) copy-start(s32[4096]{0:T(1024)} %param.23) | copy-start | bytes 49156
  378.1 32.8 %all-to-all-start.3 = ((f32[8,16,128]{2,1,0:T(8,128)}), f32[8,16,128]{2,1,0:T(8,128)S(1)}, u32[]{:S(2)}, u32[]{:S(2)}) async-start(f32[8,16,128]{2,1,0:T(8,128)} %bitcast.13), calls=%async_computation.5 | async-start | bytes 131072 | tf_op jit(solution)/shard_map/all_to_all | solution.py:159
  381.5 148.5 %all-reduce.8.cloned.1.call-start = ((), (), s32[]{:S(2)}) async-start(), calls=%async_computation.8 | async-start | bytes 131072 | tf_op jit(solution)/shard_map/psum | solution.py:171
  382.5 22.6 %copy-start.13 = (f32[1,128,128]{2,1,0:T(8,128)S(1)}, f32[1,128,128]{2,1,0:T(8,128)}, u32[]{:S(2)}) copy-start(f32[1,128,128]{2,1,0:T(8,128)} %get-tuple-element.6) | copy-start | bytes 196612
  382.5 23.9 %copy-start.12 = (f32[1,128,128]{2,1,0:T(8,128)S(1)}, f32[1,128,128]{2,1,0:T(8,128)}, u32[]{:S(2)}) copy-start(f32[1,128,128]{2,1,0:T(8,128)} %get-tuple-element.5) | copy-start | bytes 196612
  382.5 28.5 %copy-start.19 = (s32[128]{0:T(128)S(1)}, s32[128]{0:T(128)}, u32[]{:S(2)}) copy-start(s32[128]{0:T(128)} %fusion.46) | copy-start | bytes 1540
  382.6 29.8 %copy-start.18 = (pred[513]{0:T(1024)(128)(4,1)S(1)}, pred[513]{0:T(1024)(128)(4,1)}, u32[]{:S(2)}) copy-start(pred[513]{0:T(1024)(128)(4,1)} %constant.27.clone.1) | copy-start | bytes 1543
  405.1 7.4 %collective-permute-start.3 = (f32[1,128,128]{2,1,0:T(8,128)S(1)}, f32[1,128,128]{2,1,0:T(8,128)S(1)}, u32[]{:S(2)}, u32[]{:S(2)}) collective-permute-start(f32[1,128,128]{2,1,0:T(8,128)S(1)} %copy-done.13), channel_id=1, source_target_pairs={{8,0},{16,8},{24,16},{9,1},{17,9},{25,17},{10,2},{18,10},{26,18},{... | collective-permute-start | bytes 196616 | tf_op jit(solution)/shard_map/ppermute | solution.py:17
  406.4 6.4 %collective-permute-start.2 = (f32[1,128,128]{2,1,0:T(8,128)S(1)}, f32[1,128,128]{2,1,0:T(8,128)S(1)}, u32[]{:S(2)}, u32[]{:S(2)}) collective-permute-start(f32[1,128,128]{2,1,0:T(8,128)S(1)} %copy-done.12), channel_id=1, source_target_pairs={{0,8},{8,16},{16,24},{1,9},{9,17},{17,25},{2,10},{10,18},{18,26},{... | collective-permute-start | bytes 196616 | tf_op jit(solution)/shard_map/ppermute | solution.py:14
  (9 other events, 103.3 us)
Sparse Core Ops, SparseCore 0:
  81.6 34.2 reduce-scatter.2
  119.5 33.5 reduce-scatter.4
  160.8 129.3 all-reduce.9
  411.1 118.8 all-reduce.7
where the time goes:
time: 541 us; the launch traced here: 538 us
  waiting for transfers between devices  300 us (55%)
  other arithmetic  105 us (19%)
  local copies, waits for them, and re-layouts  57.1 us (11%)
  starting transfers between devices  27.1 us (5%)
  blocking collectives  17.6 us (3%)
  matrix products  16.5 us (3%)
  between operations  14.3 us (3%)
    psum x1, waiting for transfers between devices, local(): top_total = lax.psum(top_partial, ('group', 'dom'))  127 us
    psum x1, waiting for transfers between devices, local(): grad_send = lax.psum(f_weight, ('group', 'dom'))  114 us
    reduce_scatter x1, waiting for transfers between devices, local(): lax.psum_scatter(grad_partial, 'dom', scatter_dimension=0, tiled=True)  31.3 us
    scatter-add x2, other arithmetic, edge_forward(): jax.ops.segment_sum(message.astype(jnp.float32), targets, num_segments=ow...  25.4 us
    reduce_scatter x1, waiting for transfers between devices, local(): lax.psum_scatter(partial_value, 'dom', scatter_dimension=0, tiled=True)  24.4 us
    scatter-add x2, other arithmetic, edge_backward(): jax.ops.segment_sum(jnp.dot(grad_pre, w_recv.T, preferred_element_type=jn...  24.4 us
    scatter-add x2, other arithmetic, edge_backward(): jax.ops.segment_sum(jnp.dot(grad_pre, w_send.T, preferred_element_type=jn...  24.3 us
    gather x2, local copies, waits for them, and re-layouts, edge_backward(): grad_pre = (grad_sum[targets] * silu_slope(preact)).astype(jnp.bfloat16)  15.8 us
  transfers between devices with their start and end apart: 12, of which 6 were waited for; matrix products, arithmetic and copies ran while one was open for 12% of the time, Pallas kernels for 0%

commit v1 on v0

v1 whole, which is shorter than its diff:
```python
import functools

import jax
import jax.numpy as jnp
from jax import lax
from jax.experimental import pallas as pl
from jax.experimental.pallas import tpu as pltpu
from jax.sharding import PartitionSpec as P

NCC = 512
BF = jnp.bfloat16
F32 = jnp.float32
NN = ((1,), (0,))
NT = ((1,), (1,))
TN = ((0,), (0,))


def dot(a, b, dims):
    return lax.dot_general(a, b, (dims, ((), ())), preferred_element_type=F32)


def hot(row, count):
    mark = lax.broadcasted_iota(jnp.int32, (count, row.shape[1]), 0) == row
    return jnp.where(mark, 1.0, 0.0).astype(BF)


def sigmoid(v):
    return 0.5 * (1.0 + jnp.tanh(0.5 * v))


def chunk_of(edges, limit):
    size = min(edges, limit)
    while edges % size:
        size //= 2
    return size


def call(kernel, outs, *args, scratch=()):
    vmem = pl.BlockSpec(memory_space=pltpu.VMEM)
    return pl.pallas_call(
        kernel,
        out_shape=[jax.ShapeDtypeStruct(shape, kind) for shape, kind in outs],
        in_specs=[vmem] * len(args),
        out_specs=[vmem] * len(outs),
        scratch_shapes=[pltpu.VMEM(shape, kind) for shape, kind in scratch],
        compiler_params=pltpu.CompilerParams(vmem_limit_bytes=56 * 1024 * 1024),
    )(*args)


def select_kernel(index_ref, rows_ref, out_ref):
    rows = rows_ref[...]
    out_ref[...] = dot(hot(index_ref[...], rows.shape[0]), rows, TN).astype(BF)


def edges_forward(src_ref, dst_ref, send_t, recv_t, slope_ref, acc_ref, size):
    rows, count = send_t.shape[1], recv_t.shape[1]
    acc_ref[...] = jnp.zeros_like(acc_ref)

    def step(i, carry):
        at = pl.ds(pl.multiple_of(i * size, size), size)
        by_dst = hot(dst_ref[:, at], count)
        pre = dot(send_t, hot(src_ref[:, at], rows), NN) + dot(recv_t, by_dst, NN)
        sigma = sigmoid(pre)
        slope_ref[:, at] = (sigma * (1.0 + pre * (1.0 - sigma))).astype(BF)
        acc_ref[...] += dot(by_dst, (pre * sigma).astype(BF), NT)
        return carry

    lax.fori_loop(0, src_ref.shape[1] // size, step, 0)


def edges_backward(src_ref, dst_ref, grad_t, slope_ref, by_src_ref, by_dst_ref, size):
    by_src_ref[...] = jnp.zeros_like(by_src_ref)
    by_dst_ref[...] = jnp.zeros_like(by_dst_ref)

    def step(i, carry):
        at = pl.ds(pl.multiple_of(i * size, size), size)
        by_dst = hot(dst_ref[:, at], by_dst_ref.shape[0])
        gpre = (dot(grad_t, by_dst, NN) * slope_ref[:, at].astype(F32)).astype(BF)
        by_src_ref[...] += dot(hot(src_ref[:, at], by_src_ref.shape[0]), gpre, NT)
        by_dst_ref[...] += dot(by_dst, gpre, NT)
        return carry

    lax.fori_loop(0, src_ref.shape[1] // size, step, 0)


def fine_forward_kernel(
    size, src_ref, dst_ref, pool_ref, ext_ref, cot_ref, send_ref, recv_ref, node_ref,
    upd_ref, part_ref, slope_ref, acc_ref,
):
    own = ext_ref[: cot_ref.shape[0], :]
    send_t = dot(send_ref[...].T, ext_ref[...], NT).astype(BF)
    recv_t = dot(recv_ref[...].T, own, NT).astype(BF)
    edges_forward(src_ref, dst_ref, send_t, recv_t, slope_ref, acc_ref, size)
    updated = (own.astype(F32) + dot(acc_ref[...].astype(BF), node_ref[...], NN)).astype(BF)
    upd_ref[...] = updated
    both = jnp.concatenate([updated, cot_ref[...]], axis=1)
    part_ref[...] = dot(hot(pool_ref[...], part_ref.shape[0]), both, NN).astype(BF)


def coarse_forward_kernel(
    size, src_ref, dst_ref, ext_ref, sums_ref, send_ref, recv_ref, node_ref,
    mid_ref, slope_ref, acc_ref,
):
    sums = sums_ref[...]
    width = acc_ref.shape[1]
    own = (0.25 * sums[:, :width].astype(F32)).astype(BF)
    send_t = dot(send_ref[...].T, own, NT).astype(BF)
    recv_t = dot(recv_ref[...].T, own, NT).astype(BF)
    send_t = dot(send_t, hot(ext_ref[...], own.shape[0]), NN).astype(BF)
    edges_forward(src_ref, dst_ref, send_t, recv_t, slope_ref, acc_ref, size)
    mid = (own.astype(F32) + dot(acc_ref[...].astype(BF), node_ref[...], NN)).astype(BF)
    mid_ref[...] = jnp.concatenate([mid, sums[:, width:]], axis=1)


def coarse_backward_kernel(
    size, src_ref, dst_ref, ext_ref, pool_ref, mids_ref, slope_ref, top_ref, send_ref, recv_ref,
    node_ref, out_ref, by_src_ref, by_dst_ref,
):
    width = by_dst_ref.shape[1]
    own_count = by_dst_ref.shape[0]
    mids = mids_ref[...]
    own = mids[:own_count].astype(F32)
    pools = hot(pool_ref[...], NCC)
    sums = dot(pools, mids, NN)
    pooled = 0.125 * sums[:, :width]
    grad_top = sums[:, width:]
    weight = top_ref[...]
    slope_in = dot(pooled.astype(BF), weight, NN)
    sigma = sigmoid(slope_in)
    top_out = (pooled + slope_in * sigma).astype(BF)
    inner = (grad_top * (sigma * (1.0 + slope_in * (1.0 - sigma)))).astype(BF)
    grad_pool = 0.125 * (grad_top + dot(inner, weight, NT))
    both = jnp.concatenate([top_out, grad_pool.astype(BF)], axis=1)
    at_node = dot(pools[:, :own_count], both, TN)
    coarse_out = (own[:, :width] + at_node[:, :width]).astype(BF)
    grad = own[:, width:] + at_node[:, width:]
    grad_t = dot(node_ref[...], grad.astype(BF), NT).astype(BF)
    edges_backward(src_ref, dst_ref, grad_t, slope_ref, by_src_ref, by_dst_ref, size)
    by_node = dot(hot(ext_ref[...], own_count), by_src_ref[...].astype(BF), NN).astype(BF)
    grad = grad + dot(by_node, send_ref[...], NT)
    grad = grad + dot(by_dst_ref[...].astype(BF), recv_ref[...], NT)
    out_ref[...] = jnp.concatenate([coarse_out, (0.25 * grad).astype(BF)], axis=1)


def fine_backward_kernel(
    size, src_ref, dst_ref, pool_ref, ext_ref, cot_ref, upd_ref, coarse_ref, slope_ref, send_ref,
    recv_ref, node_ref, flow_ref, own_ref, halo_ref, weight_ref, by_src_ref, by_dst_ref,
):
    count, width = cot_ref.shape
    at_node = dot(hot(pool_ref[...], coarse_ref.shape[0]), coarse_ref[...], TN)
    flow_ref[...] = (upd_ref[...].astype(F32) + at_node[:, :width]).astype(BF)
    grad = cot_ref[...].astype(F32) + at_node[:, width:]
    own_ref[...] = grad
    grad_t = dot(node_ref[...], grad.astype(BF), NT).astype(BF)
    edges_backward(src_ref, dst_ref, grad_t, slope_ref, by_src_ref, by_dst_ref, size)
    by_src = by_src_ref[...].astype(BF)
    grad_ext = dot(by_src, send_ref[...], NT)
    halo_ref[...] = grad_ext[count:].astype(BF)
    own_ref[...] += grad_ext[:count] + dot(by_dst_ref[...].astype(BF), recv_ref[...], NT)
    weight_ref[...] = dot(ext_ref[...], by_src, TN).astype(BF)


def return_kernel(index_ref, rows_ref, own_ref, out_ref):
    out_ref[...] = own_ref[...] + dot(hot(index_ref[...], own_ref.shape[0]), rows_ref[...], NN)


def to_xor(value, axis, offset):
    count = lax.axis_size(axis)
    return lax.ppermute(value, axis, [(i, i ^ offset) for i in range(count)])


def xor_rows(array, by):
    count = array.shape[0]
    bit = 1
    while bit < count:
        parts = array.reshape((count // (2 * bit), 2, bit) + array.shape[1:])
        array = jnp.where((by & bit) != 0, parts[:, ::-1], parts).reshape(array.shape)
        bit *= 2
    return array


def tree_sum(parts):
    parts = [part.astype(F32) for part in parts]
    while len(parts) > 1:
        parts = [a + b for a, b in zip(parts[::2], parts[1::2])]
    return parts[0]


def exchange(blocks, other, mine):
    count, rows, width = blocks.shape
    paired = jnp.moveaxis(blocks.reshape(count // 2, 2, rows, width), 1, 0)
    if other is None:
        got = to_xor(paired[1].reshape(-1, width), "dom", 1)
    else:
        got = to_xor(jnp.concatenate([paired[1].reshape(-1, width), other]), "dom", 1)
        half = (mine.astype(F32) + got[count // 2 * rows :].astype(F32)).astype(BF)
    pieces = []
    halves = [] if other is None else [half]
    for chip in range(1, count // 2):
        message = [paired[0, chip], got[chip * rows : (chip + 1) * rows]]
        if other is not None:
            message.append(half)
        landed = to_xor(jnp.concatenate(message), "dom", 2 * chip)
        pieces.append(landed[: 2 * rows])
        if other is not None:
            halves.append(landed[2 * rows :])
    arrived = jnp.concatenate([paired[0, 0], got[:rows]] + pieces)
    return arrived, (tree_sum(halves) if other is not None else None)


def local(
    features, cotangent, fine_send, fine_rim, fine_src, fine_dst, fine_pool, coarse_send,
    coarse_src, coarse_dst, coarse_pool, w_send, w_recv, w_node, v_send, v_recv, v_node, w_top,
):
    count, width = features.shape
    doms = lax.axis_size("dom")
    groups = lax.axis_size("group")
    me = lax.axis_index("dom")
    core = me & 1
    chips = doms // 2
    slots = fine_send.shape[1]
    cslots = coarse_send.shape[1]
    rim = fine_rim.shape[1]
    coarse = coarse_pool.shape[0]
    group_coarse = coarse * doms
    half_coarse = group_coarse // 2
    edges = fine_src.shape[0]
    cedges = coarse_src.shape[0]
    forward = [(i, i + 1) for i in range(groups - 1)]
    backward = [(i + 1, i) for i in range(groups - 1)]

    def place(dom):
        return (((dom & 1) ^ core) * chips + (dom >> 1)) * coarse

    table = jnp.concatenate([coarse_send.reshape(-1), coarse_src, coarse_dst, coarse_pool])
    table = lax.all_to_all(
        jnp.broadcast_to(table[None], (doms, table.shape[0])), "dom", 0, 0, tiled=True
    )
    sends = table[:, : doms * cslots].reshape(doms, doms, cslots)
    dom_ids = jnp.arange(doms, dtype=jnp.int32)
    places = place(dom_ids)
    halo_ids = jnp.where(sends < coarse, sends + places[:, None, None], -1)
    halo_ids = jnp.swapaxes(halo_ids, 0, 1).reshape(doms, doms * cslots)
    own_ids = places[:, None] + jnp.arange(coarse, dtype=jnp.int32)[None, :]
    cext_row = jnp.concatenate([own_ids, halo_ids], axis=1).reshape(1, -1)
    cext_count = coarse + doms * cslots
    at = doms * cslots
    csrc_row = (table[:, at : at + cedges] + dom_ids[:, None] * cext_count).reshape(1, -1)
    cdst_row = (table[:, at + cedges : at + 2 * cedges] + places[:, None]).reshape(1, -1)
    pools = jnp.swapaxes(table[:, at + 2 * cedges :].reshape(chips, 2, coarse), 0, 1)
    pools = jnp.where(core == 1, pools[::-1], pools).reshape(1, group_coarse)

    halo = doms * slots
    inside = (fine_src >= count) & (fine_src < count + halo)
    device, slot = (fine_src - count) // slots, (fine_src - count) % slots
    src_row = jnp.where(inside, count + (device ^ me) * slots + slot, fine_src).reshape(1, -1)
    dst_row = fine_dst.reshape(1, -1)
    pool_row = (place(fine_pool // coarse) + fine_pool % coarse).reshape(1, -1)
    out_row = jnp.concatenate(
        [xor_rows(fine_send, me).reshape(1, -1), fine_rim.reshape(1, -1)], axis=1
    )

    (rows,) = call(select_kernel, [((halo + 2 * rim, width), BF)], out_row, features)
    incoming, _ = exchange(rows[:halo].reshape(doms, slots, width), None, None)
    from_next = lax.ppermute(rows[halo : halo + rim], "group", backward)
    from_prev = lax.ppermute(rows[halo + rim :], "group", forward)
    extended = jnp.concatenate([features, incoming, from_prev, from_next], axis=0)

    size = chunk_of(edges, 1024)
    updated, part, slope = call(
        functools.partial(fine_forward_kernel, size),
        [((count, width), BF), ((group_coarse, 2 * width), BF), ((width, edges), BF)],
        src_row, dst_row, pool_row, extended, cotangent, w_send, w_recv, w_node,
        scratch=[((count, width), F32)],
    )
    got = to_xor(part[half_coarse:], "dom", 1)
    half = (part[:half_coarse].astype(F32) + got.astype(F32)).astype(BF)
    half = tree_sum([half] + [to_xor(half, "dom", 2 * o) for o in range(1, chips)]).astype(BF)
    sums = jnp.concatenate([half, to_xor(half, "dom", 1)], axis=0)

    csize = chunk_of(cedges * doms, 512)
    mid, cslope = call(
        functools.partial(coarse_forward_kernel, csize),
        [((group_coarse, 2 * width), BF), ((width, cedges * doms), BF)],
        csrc_row, cdst_row, cext_row, sums, v_send, v_recv, v_node,
        scratch=[((group_coarse, width), F32)],
    )
    lines = half_coarse // width
    ids = pools[0, :half_coarse].reshape(lines, width)
    ids = jnp.concatenate([ids >> 7, ids & 127], axis=1).astype(BF)
    ids = jnp.concatenate([ids, jnp.zeros((-lines % 16, 2 * width), BF)], axis=0)
    message = jnp.concatenate([mid[:half_coarse], ids], axis=0)
    others = [to_xor(message, "group", o) for o in range(1, groups)]
    others = jnp.stack(others)
    others = jnp.stack([others, to_xor(others, "dom", 1)])
    ids = others[:, :, half_coarse : half_coarse + lines].astype(jnp.int32)
    ids = (ids[..., :width] * 128 + ids[..., width:]).reshape(1, -1)
    mids = jnp.concatenate([mid, others[:, :, :half_coarse].reshape(-1, 2 * width)], axis=0)
    pool_all = jnp.concatenate([pools, ids], axis=1)

    (back,) = call(
        functools.partial(coarse_backward_kernel, csize),
        [((group_coarse, 2 * width), BF)],
        csrc_row, cdst_row, cext_row, pool_all, mids, cslope, w_top, v_send, v_recv, v_node,
        scratch=[((cext_row.shape[1], width), F32), ((group_coarse, width), F32)],
    )

    flow, own, halo_grad, weight = call(
        functools.partial(fine_backward_kernel, size),
        [((count, width), BF), ((count, width), F32), ((halo + 2 * rim, width), BF),
         ((width, width), BF)],
        src_row, dst_row, pool_row, extended, cotangent, updated, back, slope, w_send, w_recv,
        w_node,
        scratch=[((extended.shape[0], width), F32), ((count, width), F32)],
    )

    low, high = weight[: width // 2], weight[width // 2 :]
    mine = jnp.where(core == 1, high, low)
    other = jnp.where(core == 1, low, high)
    returned, mine = exchange(halo_grad[:halo].reshape(doms, slots, width), other, mine)
    to_first = lax.ppermute(halo_grad[halo + rim :], "group", forward)
    to_second = lax.ppermute(halo_grad[halo : halo + rim], "group", backward)
    returned = jnp.concatenate([returned, to_first, to_second], axis=0)
    (grad_x,) = call(return_kernel, [((count, width), F32)], out_row, returned, own)

    mine = mine.astype(BF)
    mine = tree_sum([mine] + [to_xor(mine, "group", o) for o in range(1, groups)])
    other = to_xor(mine, "dom", 1)
    grad_send = jnp.concatenate(
        [jnp.where(core == 1, other, mine), jnp.where(core == 1, mine, other)], axis=0
    )
    return flow, grad_x, grad_send


def solution(mesh):
    rows = P(("group", "dom"), None)
    line = P(("group", "dom"))
    placed = (rows, rows, rows, rows, line, line, line, rows, line, line, line) + (P(),) * 7
    return jax.shard_map(
        local, mesh=mesh, in_specs=placed, out_specs=(rows, rows, P()), check_vma=False
    )
```

time: 541 us -> 104 us (0.19)
  waiting for transfers between devices: 300 us -> 17.2 us
  other arithmetic: 105 us -> 5.14 us
  local copies, waits for them, and re-layouts: 57.1 us -> 13 us
  Pallas kernels: 0 us -> 29.5 us
  blocking collectives: 17.6 us -> 0 us
  matrix products: 16.5 us -> 0 us
  between operations: 14.3 us -> 1 us
  starting transfers between devices: 27.1 us -> 37.4 us
    psum x2 -> x0, waiting for transfers between devices: 241 us -> none  [the longest x1 127 us: local(): top_total = lax.psum(top_partial, ('group', 'dom'))]
    scatter-add x13 -> x0, other arithmetic: 87.6 us -> none  [the longest x2 25.4 us: edge_forward(): jax.ops.segment_sum(message.astype(jnp.float32), targets, num_segments=ow...]
    reduce_scatter x2 -> x0, waiting for transfers between devices: 55.7 us -> none  [the longest x1 31.3 us: local(): lax.psum_scatter(grad_partial, 'dom', scatter_dimension=0, tiled=True)]
    gather x13 -> x0, local copies, waits for them, and re-layouts: 51.4 us -> none  [the longest x2 15.8 us: edge_backward(): grad_pre = (grad_sum[targets] * silu_slope(preact)).astype(jnp.bfloat16)]
    pallas_call x0 -> x6, Pallas kernels: none -> 29.5 us  [call(): pl.pallas_call(kernel, out_shape=[jax.ShapeDtypeStruct(shape, kind) for s...]
    ppermute x4 -> x25, starting transfers between devices: 12.7 us -> 32.2 us  [the longest x21 20.5 us: to_xor(): return lax.ppermute(value, axis, [(i, i ^ offset) for i in range(count)])]
    all_gather x2 -> x0, blocking collectives: 17.6 us -> none  [the longest x1 9.38 us: local(): coarse_table = lax.all_gather(coarse_out, 'dom', axis=0, tiled=True)]
    ppermute x4 -> x25, waiting for transfers between devices: 0.37 us -> 17.2 us  [the longest x21 17.2 us: to_xor(): return lax.ppermute(value, axis, [(i, i ^ offset) for i in range(count)])]
  transfers between devices with their start and end apart: 12 -> 26, of which waited for: 6 -> 13; matrix products, arithmetic and copies ran while one was open for 12% -> 5% of each run, Pallas kernels for 0% -> 4%
where the time goes in v1:
time: 104 us; the launch traced here: 103 us
  starting transfers between devices  37.4 us (36%)
  Pallas kernels  29.5 us (28%)
  waiting for transfers between devices  17.2 us (17%)
  local copies, waits for them, and re-layouts  13 us (12%)
  other arithmetic  5.14 us (5%)
    pallas_call x6, Pallas kernels, call(): pl.pallas_call(kernel, out_shape=[jax.ShapeDtypeStruct(shape, kind) for s...  29.5 us
    ppermute x21, starting transfers between devices, to_xor(): return lax.ppermute(value, axis, [(i, i ^ offset) for i in range(count)])  20.5 us
    ppermute x21, waiting for transfers between devices, to_xor(): return lax.ppermute(value, axis, [(i, i ^ offset) for i in range(count)])  17.2 us
    unnamed x41, local copies, waits for them, and re-layouts  7.62 us
    all_to_all x1, starting transfers between devices, local(): lax.all_to_all(jnp.broadcast_to(table[None], (doms, table.shape[0])), 'do...  5.2 us
    ppermute x1, starting transfers between devices, local(): from_prev = lax.ppermute(rows[halo + rim:], 'group', forward)  4.55 us
    ppermute x1, starting transfers between devices, local(): to_first = lax.ppermute(halo_grad[halo + rim:], 'group', forward)  4.55 us
  transfers between devices with their start and end apart: 26, of which 13 were waited for; matrix products, arithmetic and copies ran while one was open for 5% of the time, Pallas kernels for 4%

profile of v1, /device:TPU:0, one launch (start us, length us, event | category | flops | bytes accessed | tf_op | source)
XLA Modules:
  0.0 103.2 jit_solution(9215462410493824561)
XLA Ops:
  2.8 5.2 %all-to-all-start = ((s32[8,1,576]{2,1,0:T(1,128)}), s32[8,1,576]{2,1,0:T(1,128)S(1)}, u32[]{:S(2)}, u32[]{:S(2)}) async-start(s32[8,1,576]{2,1,0:T(1,128)} %broadcast_in_dim.8), calls=%async_computation | async-start | bytes 40960 | tf_op jit(solution)/shard_map/all_to_all | solution.py:236
  10.1 1.9 %shard_map.193 = bf16[384,128]{1,0:T(8,128)(2,1)} custom-call(s32[1,384]{1,0:T(1,128)} %pad_add_fusion.3.index_ref, bf16[512,128]{1,0:T(8,128)(2,1)} %rows_ref.1), custom_call_target="tpu_custom_call" | custom-call | tf_op jit(solution)/shard_map/pallas_call | solution.py:40
  14.7 4.5 %collective-permute-start.4 = (bf16[128,128]{1,0:T(8,128)(2,1)S(1)}, bf16[128,128]{1,0:T(8,128)(2,1)S(1)}, u32[]{:S(2)}, u32[]{:S(2)}) collective-permute-start(bf16[128,128]{1,0:T(8,128)(2,1)S(1)} %get-tuple-element.27), channel_id=1, source_target_pairs={{0,8},{8,16},{16,24},{1,9},{9,17},{17,25},{2,10},{10,18},{18,26},{... | collective-permute-start | bytes 98312 | tf_op jit(solution)/shard_map/ppermute | solution.py:266
  22.2 1.7 %collective-permute-start.1 = (bf16[32,128]{1,0:T(8,128)(2,1)S(1)}, bf16[32,128]{1,0:T(8,128)(2,1)S(1)}, u32[]{:S(2)}, u32[]{:S(2)}) collective-permute-start(bf16[32,128]{1,0:T(8,128)(2,1)S(1)} %pad_maximum_fusion.9), channel_id=1, source_target_pairs={{0,2},{1,3},{2,0},{3,1},{4,6},{5,7},{6,4},{7,5},{8,10},{9,11},{10,... | collective-permute-start | bytes 24584 | tf_op jit(solution)/shard_map/ppermute | solution.py:169
  23.9 1.5 %collective-permute-start.2 = (bf16[32,128]{1,0:T(8,128)(2,1)S(1)}, bf16[32,128]{1,0:T(8,128)(2,1)S(1)}, u32[]{:S(2)}, u32[]{:S(2)}) collective-permute-start(bf16[32,128]{1,0:T(8,128)(2,1)S(1)} %pad_maximum_fusion.10), channel_id=1, source_target_pairs={{0,4},{1,5},{2,6},{3,7},{4,0},{5,1},{6,2},{7,3},{8,12},{9,13},{10,... | collective-permute-start | bytes 24584 | tf_op jit(solution)/shard_map/ppermute | solution.py:169
  26.0 1.6 %collective-permute-done.2 = bf16[32,128]{1,0:T(8,128)(2,1)S(1)} collective-permute-done((bf16[32,128]{1,0:T(8,128)(2,1)S(1)}, bf16[32,128]{1,0:T(8,128)(2,1)S(1)}, u32[]{:S(2)}, u32[]{:S(2)}) %collective-permute-start.2) | collective-permute-done | bytes 8224 | tf_op jit(solution)/shard_map/ppermute | solution.py:169
  27.6 2.4 %collective-permute-done.3 = bf16[32,128]{1,0:T(8,128)(2,1)S(1)} collective-permute-done((bf16[32,128]{1,0:T(8,128)(2,1)S(1)}, bf16[32,128]{1,0:T(8,128)(2,1)S(1)}, u32[]{:S(2)}, u32[]{:S(2)}) %collective-permute-start.3) | collective-permute-done | bytes 8224 | tf_op jit(solution)/shard_map/ppermute | solution.py:169
  30.7 7.3 %shard_map.194 = (bf16[512,128]{1,0:T(8,128)(2,1)}, bf16[256,256]{1,0:T(8,128)(2,1)}, bf16[128,4096]{1,0:T(8,128)(2,1)}) custom-call(s32[1,4096]{1,0:T(1,128)} %bitcast.72, s32[1,4096]{1,0:T(1,128)} %bitcast.91, s32[1,512]{1,0:T(1,128)} %bitcast.98, bf16[896,128]{1,0:T(8,128)(2,1)} %copy-done, bf16[512,128]{1,0:T(8,128)(2,1)} %cot_ref.3, ...), custom_call_target="tpu_custom_call" | custom-call | tf_op jit(solution)/shard_map/pallas_call | solution.py:40
  40.6 1.6 %collective-permute-start.8 = (bf16[128,256]{1,0:T(8,128)(2,1)S(1)}, bf16[128,256]{1,0:T(8,128)(2,1)S(1)}, u32[]{:S(2)}, u32[]{:S(2)}) collective-permute-start(bf16[128,256]{1,0:T(8,128)(2,1)S(1)} %add_convert_fusion.1), channel_id=1, source_target_pairs={{0,4},{1,5},{2,6},{3,7},{4,0},{5,1},{6,2},{7,3},{8,12},{9,13},{10,... | collective-permute-start | bytes 196616 | tf_op jit(solution)/shard_map/ppermute | solution.py:169
  42.3 1.5 %collective-permute-start.7 = (bf16[128,256]{1,0:T(8,128)(2,1)S(1)}, bf16[128,256]{1,0:T(8,128)(2,1)S(1)}, u32[]{:S(2)}, u32[]{:S(2)}) collective-permute-start(bf16[128,256]{1,0:T(8,128)(2,1)S(1)} %add_convert_fusion.1), channel_id=1, source_target_pairs={{0,2},{1,3},{2,0},{3,1},{4,6},{5,7},{6,4},{7,5},{8,10},{9,11},{10,... | collective-permute-start | bytes 196616 | tf_op jit(solution)/shard_map/ppermute | solution.py:169
  48.6 4.3 %shard_map.195 = (bf16[256,256]{1,0:T(8,128)(2,1)}, bf16[128,2048]{1,0:T(8,128)(2,1)}) custom-call(s32[1,2048]{1,0:T(1,128)} %bitcast.86, s32[1,2048]{1,0:T(1,128)} %bitcast.84, s32[1,512]{1,0:T(1,128)} %reshape.120.ext_ref, bf16[256,256]{1,0:T(8,128)(2,1)} %pad_maximum_fusion.3.sums_ref, bf16[128,128]{1,0:T(8,128)(2,1)} %send_ref.6, ...), custom_call_target="tpu_custom_call" | custom-call | tf_op jit(solution)/shard_map/pallas_call | solution.py:40
  53.8 1.5 %collective-permute-start.13 = (bf16[144,256]{1,0:T(8,128)(2,1)S(1)}, bf16[144,256]{1,0:T(8,128)(2,1)S(1)}, u32[]{:S(2)}, u32[]{:S(2)}) collective-permute-start(bf16[144,256]{1,0:T(8,128)(2,1)S(1)} %maximum_maximum_fusion), channel_id=1, source_target_pairs={{0,24},{8,16},{16,8},{24,0},{1,25},{9,17},{17,9},{25,1},{2,26},{10... | collective-permute-start | bytes 221192 | tf_op jit(solution)/shard_map/ppermute | solution.py:169
  55.3 1.6 %collective-permute-start.12 = (bf16[144,256]{1,0:T(8,128)(2,1)S(1)}, bf16[144,256]{1,0:T(8,128)(2,1)S(1)}, u32[]{:S(2)}, u32[]{:S(2)}) collective-permute-start(bf16[144,256]{1,0:T(8,128)(2,1)S(1)} %maximum_maximum_fusion), channel_id=1, source_target_pairs={{0,16},{8,24},{16,0},{24,8},{1,17},{9,25},{17,1},{25,9},{2,18},{10... | collective-permute-start | bytes 221192 | tf_op jit(solution)/shard_map/ppermute | solution.py:169
  58.3 2.0 %collective-permute-done.13 = bf16[144,256]{1,0:T(8,128)(2,1)S(1)} collective-permute-done((bf16[144,256]{1,0:T(8,128)(2,1)S(1)}, bf16[144,256]{1,0:T(8,128)(2,1)S(1)}, u32[]{:S(2)}, u32[]{:S(2)}) %collective-permute-start.13) | collective-permute-done | bytes 73760 | tf_op jit(solution)/shard_map/ppermute | solution.py:169
  60.3 3.7 %collective-permute-done.12 = bf16[144,256]{1,0:T(8,128)(2,1)S(1)} collective-permute-done((bf16[144,256]{1,0:T(8,128)(2,1)S(1)}, bf16[144,256]{1,0:T(8,128)(2,1)S(1)}, u32[]{:S(2)}, u32[]{:S(2)}) %collective-permute-start.12) | collective-permute-done | bytes 73760 | tf_op jit(solution)/shard_map/ppermute | solution.py:169
  64.1 1.5 %collective-permute-done.14 = bf16[3,144,256]{2,1,0:T(8,128)(2,1)S(1)} collective-permute-done((bf16[3,144,256]{2,1,0:T(8,128)(2,1)S(1)}, bf16[3,144,256]{2,1,0:T(8,128)(2,1)S(1)}, u32[]{:S(2)}, u32[]{:S(2)}) %collective-permute-start.14) | collective-permute-done | bytes 221216 | tf_op jit(solution)/shard_map/ppermute | solution.py:169
  67.3 5.9 %shard_map.196.coarse_ref = bf16[256,256]{1,0:T(8,128)(2,1)} custom-call(s32[1,2048]{1,0:T(1,128)} %bitcast.87, s32[1,2048]{1,0:T(1,128)} %bitcast.85, s32[1,512]{1,0:T(1,128)} %reshape.120.ext_ref, s32[1,1024]{1,0:T(1,128)} %pad_add_fusion.2.pool_ref, bf16[1024,256]{1,0:T(8,128)(2,1)} %pad_maximum_fusion.mids_ref, ...), custom_call_target="tpu_custom_call" | custom-call | tf_op jit(solution)/shard_map/pallas_call | solution.py:40
  73.2 8.2 %shard_map.197 = (bf16[512,128]{1,0:T(8,128)(2,1)}, f32[512,128]{1,0:T(8,128)}, bf16[384,128]{1,0:T(8,128)(2,1)}, bf16[128,128]{1,0:T(8,128)(2,1)}) custom-call(s32[1,4096]{1,0:T(1,128)} %bitcast.73, s32[1,4096]{1,0:T(1,128)} %bitcast.92, s32[1,512]{1,0:T(1,128)} %bitcast.99, bf16[896,128]{1,0:T(8,128)(2,1)} %copy-done, bf16[512,128]{1,0:T(8,128)(2,1)} %cot_ref.3, ...), custom_call_target="tpu_custom_call" | custom-call | tf_op jit(solution)/shard_map/pallas_call | solution.py:40
  84.2 1.5 %collective-permute-start.18 = (bf16[96,128]{1,0:T(8,128)(2,1)S(1)}, bf16[96,128]{1,0:T(8,128)(2,1)S(1)}, u32[]{:S(2)}, u32[]{:S(2)}) collective-permute-start(bf16[96,128]{1,0:T(8,128)(2,1)S(1)} %get-tuple-element.45), channel_id=1, source_target_pairs={{0,6},{1,7},{2,4},{3,5},{4,2},{5,3},{6,0},{7,1},{8,14},{9,15},{10,... | collective-permute-start | bytes 73736 | tf_op jit(solution)/shard_map/ppermute | solution.py:169
  85.8 1.5 %collective-permute-start.17 = (bf16[96,128]{1,0:T(8,128)(2,1)S(1)}, bf16[96,128]{1,0:T(8,128)(2,1)S(1)}, u32[]{:S(2)}, u32[]{:S(2)}) collective-permute-start(bf16[96,128]{1,0:T(8,128)(2,1)S(1)} %get-tuple-element.46), channel_id=1, source_target_pairs={{0,4},{1,5},{2,6},{3,7},{4,0},{5,1},{6,2},{7,3},{8,12},{9,13},{10,... | collective-permute-start | bytes 73736 | tf_op jit(solution)/shard_map/ppermute | solution.py:169
  89.1 4.5 %collective-permute-start.19 = (bf16[128,128]{1,0:T(8,128)(2,1)S(1)}, bf16[128,128]{1,0:T(8,128)(2,1)S(1)}, u32[]{:S(2)}, u32[]{:S(2)}) collective-permute-start(bf16[128,128]{1,0:T(8,128)(2,1)S(1)} %get-tuple-element.24), channel_id=1, source_target_pairs={{0,8},{8,16},{16,24},{1,9},{9,17},{17,25},{2,10},{10,18},{18,26},{... | collective-permute-start | bytes 98312 | tf_op jit(solution)/shard_map/ppermute | solution.py:321
  93.8 1.5 %collective-permute-start.22 = (bf16[64,128]{1,0:T(8,128)(2,1)S(1)}, bf16[64,128]{1,0:T(8,128)(2,1)S(1)}, u32[]{:S(2)}, u32[]{:S(2)}) collective-permute-start(bf16[64,128]{1,0:T(8,128)(2,1)S(1)} %add_convert_fusion.2), channel_id=1, source_target_pairs={{0,16},{8,24},{16,0},{24,8},{1,17},{9,25},{17,1},{25,9},{2,18},{10... | collective-permute-start | bytes 49160 | tf_op jit(solution)/shard_map/ppermute | solution.py:169
  95.2 2.9 %collective-permute-start.21 = (bf16[64,128]{1,0:T(8,128)(2,1)S(1)}, bf16[64,128]{1,0:T(8,128)(2,1)S(1)}, u32[]{:S(2)}, u32[]{:S(2)}) collective-permute-start(bf16[64,128]{1,0:T(8,128)(2,1)S(1)} %add_convert_fusion.2), channel_id=1, source_target_pairs={{0,8},{8,0},{16,24},{24,16},{1,9},{9,1},{17,25},{25,17},{2,10},{10... | collective-permute-start | bytes 49160 | tf_op jit(solution)/shard_map/ppermute | solution.py:169
  100.6 2.0 %shard_map.198 = f32[512,128]{1,0:T(8,128)} custom-call(s32[1,384]{1,0:T(1,128)} %pad_add_fusion.3.index_ref, bf16[384,128]{1,0:T(8,128)(2,1)} %copy-done.5, f32[512,128]{1,0:T(8,128)} %get-tuple-element.20.own_ref), custom_call_target="tpu_custom_call" | custom-call | tf_op jit(solution)/shard_map/pallas_call | solution.py:40
  (138 shorter events, 30.6 us)
Async XLA Ops:
  2.8 19.2 %all-to-all-start = ((s32[8,1,576]{2,1,0:T(1,128)}), s32[8,1,576]{2,1,0:T(1,128)S(1)}, u32[]{:S(2)}, u32[]{:S(2)}) async-start(s32[8,1,576]{2,1,0:T(1,128)} %broadcast_in_dim.8), calls=%async_computation | async-start | bytes 40960 | tf_op jit(solution)/shard_map/all_to_all | solution.py:236
  12.8 9.4 %collective-permute-start = (bf16[64,128]{1,0:T(8,128)(2,1)S(1)}, bf16[64,128]{1,0:T(8,128)(2,1)S(1)}, u32[]{:S(2)}, u32[]{:S(2)}) collective-permute-start(bf16[64,128]{1,0:T(8,128)(2,1)S(1)} %bitcast.106), channel_id=1, source_target_pairs={{0,1},{1,0},{2,3},{3,2},{4,5},{5,4},{6,7},{7,6},{8,9},{9,8},{10,11... | collective-permute-start | bytes 49160 | tf_op jit(solution)/shard_map/ppermute | solution.py:169
  13.4 16.6 %collective-permute-start.5 = (bf16[128,128]{1,0:T(8,128)(2,1)S(1)}, bf16[128,128]{1,0:T(8,128)(2,1)S(1)}, u32[]{:S(2)}, u32[]{:S(2)}) collective-permute-start(bf16[128,128]{1,0:T(8,128)(2,1)S(1)} %get-tuple-element.26), channel_id=1, source_target_pairs={{8,0},{16,8},{24,16},{9,1},{17,9},{25,17},{10,2},{18,10},{26,18},{... | collective-permute-start | bytes 98312 | tf_op jit(solution)/shard_map/ppermute | solution.py:265
  14.7 15.3 %collective-permute-start.4 = (bf16[128,128]{1,0:T(8,128)(2,1)S(1)}, bf16[128,128]{1,0:T(8,128)(2,1)S(1)}, u32[]{:S(2)}, u32[]{:S(2)}) collective-permute-start(bf16[128,128]{1,0:T(8,128)(2,1)S(1)} %get-tuple-element.27), channel_id=1, source_target_pairs={{0,8},{8,16},{16,24},{1,9},{9,17},{17,25},{2,10},{10,18},{18,26},{... | collective-permute-start | bytes 98312 | tf_op jit(solution)/shard_map/ppermute | solution.py:266
  22.2 3.7 %collective-permute-start.1 = (bf16[32,128]{1,0:T(8,128)(2,1)S(1)}, bf16[32,128]{1,0:T(8,128)(2,1)S(1)}, u32[]{:S(2)}, u32[]{:S(2)}) collective-permute-start(bf16[32,128]{1,0:T(8,128)(2,1)S(1)} %pad_maximum_fusion.9), channel_id=1, source_target_pairs={{0,2},{1,3},{2,0},{3,1},{4,6},{5,7},{6,4},{7,5},{8,10},{9,11},{10,... | collective-permute-start | bytes 24584 | tf_op jit(solution)/shard_map/ppermute | solution.py:169
  23.9 3.7 %collective-permute-start.2 = (bf16[32,128]{1,0:T(8,128)(2,1)S(1)}, bf16[32,128]{1,0:T(8,128)(2,1)S(1)}, u32[]{:S(2)}, u32[]{:S(2)}) collective-permute-start(bf16[32,128]{1,0:T(8,128)(2,1)S(1)} %pad_maximum_fusion.10), channel_id=1, source_target_pairs={{0,4},{1,5},{2,6},{3,7},{4,0},{5,1},{6,2},{7,3},{8,12},{9,13},{10,... | collective-permute-start | bytes 24584 | tf_op jit(solution)/shard_map/ppermute | solution.py:169
  25.4 4.5 %collective-permute-start.3 = (bf16[32,128]{1,0:T(8,128)(2,1)S(1)}, bf16[32,128]{1,0:T(8,128)(2,1)S(1)}, u32[]{:S(2)}, u32[]{:S(2)}) collective-permute-start(bf16[32,128]{1,0:T(8,128)(2,1)S(1)} %pad_maximum_fusion.11), channel_id=1, source_target_pairs={{0,6},{1,7},{2,4},{3,5},{4,2},{5,3},{6,0},{7,1},{8,14},{9,15},{10,... | collective-permute-start | bytes 24584 | tf_op jit(solution)/shard_map/ppermute | solution.py:169
  40.2 5.8 %collective-permute-start.9 = (bf16[128,256]{1,0:T(8,128)(2,1)S(1)}, bf16[128,256]{1,0:T(8,128)(2,1)S(1)}, u32[]{:S(2)}, u32[]{:S(2)}) collective-permute-start(bf16[128,256]{1,0:T(8,128)(2,1)S(1)} %add_convert_fusion.1), channel_id=1, source_target_pairs={{0,6},{1,7},{2,4},{3,5},{4,2},{5,3},{6,0},{7,1},{8,14},{9,15},{10,... | collective-permute-start | bytes 196616 | tf_op jit(solution)/shard_map/ppermute | solution.py:169
  40.6 5.4 %collective-permute-start.8 = (bf16[128,256]{1,0:T(8,128)(2,1)S(1)}, bf16[128,256]{1,0:T(8,128)(2,1)S(1)}, u32[]{:S(2)}, u32[]{:S(2)}) collective-permute-start(bf16[128,256]{1,0:T(8,128)(2,1)S(1)} %add_convert_fusion.1), channel_id=1, source_target_pairs={{0,4},{1,5},{2,6},{3,7},{4,0},{5,1},{6,2},{7,3},{8,12},{9,13},{10,... | collective-permute-start | bytes 196616 | tf_op jit(solution)/shard_map/ppermute | solution.py:169
  42.3 4.3 %collective-permute-start.7 = (bf16[128,256]{1,0:T(8,128)(2,1)S(1)}, bf16[128,256]{1,0:T(8,128)(2,1)S(1)}, u32[]{:S(2)}, u32[]{:S(2)}) collective-permute-start(bf16[128,256]{1,0:T(8,128)(2,1)S(1)} %add_convert_fusion.1), channel_id=1, source_target_pairs={{0,2},{1,3},{2,0},{3,1},{4,6},{5,7},{6,4},{7,5},{8,10},{9,11},{10,... | collective-permute-start | bytes 196616 | tf_op jit(solution)/shard_map/ppermute | solution.py:169
  46.6 1.3 %collective-permute-start.10 = (bf16[128,256]{1,0:T(8,128)(2,1)S(1)}, bf16[128,256]{1,0:T(8,128)(2,1)S(1)}, u32[]{:S(2)}, u32[]{:S(2)}) collective-permute-start(bf16[128,256]{1,0:T(8,128)(2,1)S(1)} %add_convert_fusion), channel_id=1, source_target_pairs={{0,1},{1,0},{2,3},{3,2},{4,5},{5,4},{6,7},{7,6},{8,9},{9,8},{10,11... | collective-permute-start | bytes 196616 | tf_op jit(solution)/shard_map/ppermute | solution.py:169
  53.8 6.5 %collective-permute-start.13 = (bf16[144,256]{1,0:T(8,128)(2,1)S(1)}, bf16[144,256]{1,0:T(8,128)(2,1)S(1)}, u32[]{:S(2)}, u32[]{:S(2)}) collective-permute-start(bf16[144,256]{1,0:T(8,128)(2,1)S(1)} %maximum_maximum_fusion), channel_id=1, source_target_pairs={{0,24},{8,16},{16,8},{24,0},{1,25},{9,17},{17,9},{25,1},{2,26},{10... | collective-permute-start | bytes 221192 | tf_op jit(solution)/shard_map/ppermute | solution.py:169
  55.3 8.7 %collective-permute-start.12 = (bf16[144,256]{1,0:T(8,128)(2,1)S(1)}, bf16[144,256]{1,0:T(8,128)(2,1)S(1)}, u32[]{:S(2)}, u32[]{:S(2)}) collective-permute-start(bf16[144,256]{1,0:T(8,128)(2,1)S(1)} %maximum_maximum_fusion), channel_id=1, source_target_pairs={{0,16},{8,24},{16,0},{24,8},{1,17},{9,25},{17,1},{25,9},{2,18},{10... | collective-permute-start | bytes 221192 | tf_op jit(solution)/shard_map/ppermute | solution.py:169
  57.0 7.0 %collective-permute-start.11 = (bf16[144,256]{1,0:T(8,128)(2,1)S(1)}, bf16[144,256]{1,0:T(8,128)(2,1)S(1)}, u32[]{:S(2)}, u32[]{:S(2)}) collective-permute-start(bf16[144,256]{1,0:T(8,128)(2,1)S(1)} %maximum_maximum_fusion), channel_id=1, source_target_pairs={{0,8},{8,0},{16,24},{24,16},{1,9},{9,1},{17,25},{25,17},{2,10},{10... | collective-permute-start | bytes 221192 | tf_op jit(solution)/shard_map/ppermute | solution.py:169
  64.0 1.5 %collective-permute-start.14 = (bf16[3,144,256]{2,1,0:T(8,128)(2,1)S(1)}, bf16[3,144,256]{2,1,0:T(8,128)(2,1)S(1)}, u32[]{:S(2)}, u32[]{:S(2)}) collective-permute-start(bf16[3,144,256]{2,1,0:T(8,128)(2,1)S(1)} %get-tuple-element.22), channel_id=1, source_target_pairs={{0,1},{1,0},{2,3},{3,2},{4,5},{5,4},{6,7},{7,6},{8,9},{9,8},{10,11... | collective-permute-start | bytes 663560 | tf_op jit(solution)/shard_map/ppermute | solution.py:169
  84.2 9.4 %collective-permute-start.18 = (bf16[96,128]{1,0:T(8,128)(2,1)S(1)}, bf16[96,128]{1,0:T(8,128)(2,1)S(1)}, u32[]{:S(2)}, u32[]{:S(2)}) collective-permute-start(bf16[96,128]{1,0:T(8,128)(2,1)S(1)} %get-tuple-element.45), channel_id=1, source_target_pairs={{0,6},{1,7},{2,4},{3,5},{4,2},{5,3},{6,0},{7,1},{8,14},{9,15},{10,... | collective-permute-start | bytes 73736 | tf_op jit(solution)/shard_map/ppermute | solution.py:169
  85.8 7.9 %collective-permute-start.17 = (bf16[96,128]{1,0:T(8,128)(2,1)S(1)}, bf16[96,128]{1,0:T(8,128)(2,1)S(1)}, u32[]{:S(2)}, u32[]{:S(2)}) collective-permute-start(bf16[96,128]{1,0:T(8,128)(2,1)S(1)} %get-tuple-element.46), channel_id=1, source_target_pairs={{0,4},{1,5},{2,6},{3,7},{4,0},{5,1},{6,2},{7,3},{8,12},{9,13},{10,... | collective-permute-start | bytes 73736 | tf_op jit(solution)/shard_map/ppermute | solution.py:169
  87.2 6.4 %collective-permute-start.16 = (bf16[96,128]{1,0:T(8,128)(2,1)S(1)}, bf16[96,128]{1,0:T(8,128)(2,1)S(1)}, u32[]{:S(2)}, u32[]{:S(2)}) collective-permute-start(bf16[96,128]{1,0:T(8,128)(2,1)S(1)} %get-tuple-element.47), channel_id=1, source_target_pairs={{0,2},{1,3},{2,0},{3,1},{4,6},{5,7},{6,4},{7,5},{8,10},{9,11},{10,... | collective-permute-start | bytes 73736 | tf_op jit(solution)/shard_map/ppermute | solution.py:169
  87.8 12.2 %collective-permute-start.20 = (bf16[128,128]{1,0:T(8,128)(2,1)S(1)}, bf16[128,128]{1,0:T(8,128)(2,1)S(1)}, u32[]{:S(2)}, u32[]{:S(2)}) collective-permute-start(bf16[128,128]{1,0:T(8,128)(2,1)S(1)} %get-tuple-element.23), channel_id=1, source_target_pairs={{8,0},{16,8},{24,16},{9,1},{17,9},{25,17},{10,2},{18,10},{26,18},{... | collective-permute-start | bytes 98312 | tf_op jit(solution)/shard_map/ppermute | solution.py:322
  89.1 9.1 %collective-permute-start.19 = (bf16[128,128]{1,0:T(8,128)(2,1)S(1)}, bf16[128,128]{1,0:T(8,128)(2,1)S(1)}, u32[]{:S(2)}, u32[]{:S(2)}) collective-permute-start(bf16[128,128]{1,0:T(8,128)(2,1)S(1)} %get-tuple-element.24), channel_id=1, source_target_pairs={{0,8},{8,16},{16,24},{1,9},{9,17},{17,25},{2,10},{10,18},{18,26},{... | collective-permute-start | bytes 98312 | tf_op jit(solution)/shard_map/ppermute | solution.py:321
  93.7 5.6 %collective-permute-start.23 = (bf16[64,128]{1,0:T(8,128)(2,1)S(1)}, bf16[64,128]{1,0:T(8,128)(2,1)S(1)}, u32[]{:S(2)}, u32[]{:S(2)}) collective-permute-start(bf16[64,128]{1,0:T(8,128)(2,1)S(1)} %add_convert_fusion.2), channel_id=1, source_target_pairs={{0,24},{8,16},{16,8},{24,0},{1,25},{9,17},{17,9},{25,1},{2,26},{10... | collective-permute-start | bytes 49160 | tf_op jit(solution)/shard_map/ppermute | solution.py:169
  93.8 5.5 %collective-permute-start.22 = (bf16[64,128]{1,0:T(8,128)(2,1)S(1)}, bf16[64,128]{1,0:T(8,128)(2,1)S(1)}, u32[]{:S(2)}, u32[]{:S(2)}) collective-permute-start(bf16[64,128]{1,0:T(8,128)(2,1)S(1)} %add_convert_fusion.2), channel_id=1, source_target_pairs={{0,16},{8,24},{16,0},{24,8},{1,17},{9,25},{17,1},{25,9},{2,18},{10... | collective-permute-start | bytes 49160 | tf_op jit(solution)/shard_map/ppermute | solution.py:169
  95.2 4.6 %collective-permute-start.21 = (bf16[64,128]{1,0:T(8,128)(2,1)S(1)}, bf16[64,128]{1,0:T(8,128)(2,1)S(1)}, u32[]{:S(2)}, u32[]{:S(2)}) collective-permute-start(bf16[64,128]{1,0:T(8,128)(2,1)S(1)} %add_convert_fusion.2), channel_id=1, source_target_pairs={{0,8},{8,0},{16,24},{24,16},{1,9},{9,1},{17,25},{25,17},{2,10},{10... | collective-permute-start | bytes 49160 | tf_op jit(solution)/shard_map/ppermute | solution.py:169
  99.9 2.7 %collective-permute-start.24 = (f32[64,128]{1,0:T(8,128)S(1)}, f32[64,128]{1,0:T(8,128)S(1)}, u32[]{:S(2)}, u32[]{:S(2)}) collective-permute-start(f32[64,128]{1,0:T(8,128)S(1)} %add_add_fusion), channel_id=1, source_target_pairs={{0,1},{1,0},{2,3},{3,2},{4,5},{5,4},{6,7},{7,6},{8,9},{9,8},{10,11... | collective-permute-start | bytes 98312 | tf_op jit(solution)/shard_map/ppermute | solution.py:169
  (15 other events, 19.8 us)

commit v2 on v1

v2 whole, which is shorter than its diff:
```python
import functools

import jax
import jax.numpy as jnp
from jax import lax
from jax.experimental import pallas as pl
from jax.experimental.pallas import tpu as pltpu
from jax.sharding import PartitionSpec as P

NCC = 512
BF = jnp.bfloat16
F32 = jnp.float32
NN = ((1,), (0,))
NT = ((1,), (1,))
TN = ((0,), (0,))


def dot(a, b, dims):
    return lax.dot_general(a, b, (dims, ((), ())), preferred_element_type=F32)


def hot(row, count):
    mark = lax.broadcasted_iota(jnp.int32, (count, row.shape[1]), 0) == row
    return jnp.where(mark, 1.0, 0.0).astype(BF)


def sigmoid(v):
    return 0.5 * (1.0 + jnp.tanh(0.5 * v))


def chunk_of(edges, limit):
    size = min(edges, limit)
    while edges % size:
        size //= 2
    return size


def whole(count):
    return [pl.BlockSpec(memory_space=pltpu.VMEM)] * count


def call(kernel, outs, *args, scratch=(), extra=0):
    return pl.pallas_call(
        kernel,
        out_shape=[jax.ShapeDtypeStruct(shape, kind) for shape, kind in outs],
        in_specs=whole(len(args)),
        out_specs=whole(len(outs)),
        scratch_shapes=[pltpu.VMEM(shape, kind) for shape, kind in scratch],
        compiler_params=pltpu.CompilerParams(vmem_limit_bytes=(14 << 20) + extra),
    )(*args)


def log2(value):
    assert value & (value - 1) == 0
    return value.bit_length() - 1


def lanes(count, rows=1):
    return lax.broadcasted_iota(jnp.int32, (rows, count), 1)


def order(dom, chips):
    return (dom & 1) * chips + (dom >> 1)


def place(dom, core, chips):
    return ((dom & 1) ^ core) * chips + (dom >> 1)


def tree_sum(parts):
    parts = [part.astype(F32) for part in parts]
    while len(parts) > 1:
        parts = [a + b for a, b in zip(parts[::2], parts[1::2])]
    return parts[0]


class Payload:
    def __init__(self, cedges, group_coarse, doms):
        self.edges = cedges // 128
        self.lines = group_coarse // 128
        self.dst = self.edges
        self.high = 2 * self.edges
        self.low = self.high + self.lines
        self.send = self.low + self.lines
        self.rows = -(-(self.send + doms) // 16) * 16


def send_row(send_ref):
    doms, slots = send_ref.shape
    send = send_ref[...]
    spot = lax.broadcasted_iota(jnp.int32, (slots, doms * slots), 0)
    spread = jnp.where(lanes(doms * slots, slots) & (slots - 1) == spot, 1.0, 0.0).astype(BF)
    high = dot((send >> 4).astype(F32).astype(BF), spread, NN)
    low = dot((send & 15).astype(F32).astype(BF), spread, NN)
    value = high * 16.0 + low
    owner = lax.broadcasted_iota(jnp.int32, (doms, doms * slots), 0)
    mine = lanes(doms * slots, doms) >> log2(slots) == owner
    return jnp.sum(jnp.where(mine, value, 0.0), axis=0, keepdims=True).astype(jnp.int32)


def start_kernel(
    pay, send_ref, rim_ref, rows_ref, csrc_ref, cdst_ref, cpool_ref, csend_ref,
    odd_ref, even_ref, pay_ref, first_ref, second_ref, picked_ref, lines_ref,
):
    me = lax.axis_index("dom")
    doms, slots = send_ref.shape
    rows = rows_ref[...]
    count = rows.shape[0]
    picked_ref[...] = dot(hot(send_row(send_ref), count), rows, TN).astype(BF)
    for chip in range(doms // 2):
        here = pl.ds(chip * slots, slots)
        for part, ref in ((0, even_ref), (1, odd_ref)):
            at = pl.multiple_of(((2 * chip + part) ^ me) * slots, slots)
            ref[here, :] = picked_ref[pl.ds(at, slots), :]
    first_ref[...] = dot(hot(rim_ref[0:1, :], count), rows, TN).astype(BF)
    second_ref[...] = dot(hot(rim_ref[1:2, :], count), rows, TN).astype(BF)

    lines_ref[...] = jnp.zeros_like(lines_ref)
    lines_ref[: pay.edges, :] = csrc_ref[...].astype(F32)
    lines_ref[pay.dst : pay.dst + pay.edges, :] = cdst_ref[...].astype(F32)
    coarse = cpool_ref.shape[1]
    cslots = csend_ref.shape[1]
    pool = cpool_ref[...]
    spot = lax.broadcasted_iota(jnp.int32, (coarse, pay.lines * 128), 0)
    at = order(me, doms // 2) * coarse
    spread = jnp.where(lanes(pay.lines * 128, coarse) == spot + at, 1.0, 0.0).astype(BF)
    high = dot((pool >> 7).astype(F32).astype(BF), spread, NN)
    low = dot((pool & 127).astype(F32).astype(BF), spread, NN)
    for line in range(pay.lines):
        here = slice(line * 128, line * 128 + 128)
        lines_ref[pay.high + line : pay.high + line + 1, :] = high[:, here]
        lines_ref[pay.low + line : pay.low + line + 1, :] = low[:, here]
    spot = lax.broadcasted_iota(jnp.int32, (cslots, 128), 0)
    spread = jnp.where(lanes(128, cslots) == spot + me * cslots, 1.0, 0.0).astype(BF)
    sends = dot(csend_ref[...].astype(F32).astype(BF), spread, NN)
    lines_ref[pay.send : pay.send + doms, :] = sends
    payload = lines_ref[...].astype(BF)
    pay_ref[...] = payload
    odd_ref[doms // 2 * slots :, :] = payload


def pack_kernel(slots, even_ref, got_ref, pay_ref, *out_refs):
    chips = len(out_refs) + 1
    for chip, ref in enumerate(out_refs, 1):
        ref[:slots, :] = even_ref[chip * slots : chip * slots + slots, :]
        ref[slots : 2 * slots, :] = got_ref[chip * slots : chip * slots + slots, :]
        rows = pay_ref.shape[0]
        ref[2 * slots : 2 * slots + rows, :] = pay_ref[...]
        if ref.shape[0] > 2 * slots + rows:
            ref[2 * slots + rows :, :] = got_ref[chips * slots :, :]


def edges_forward(src_ref, dst_ref, send_t, recv_t, slope_ref, acc_ref, size):
    rows, count = send_t.shape[1], recv_t.shape[1]
    acc_ref[...] = jnp.zeros_like(acc_ref)

    def step(i, carry):
        at = pl.ds(pl.multiple_of(i * size, size), size)
        by_dst = hot(dst_ref[:, at], count)
        pre = dot(send_t, hot(src_ref[:, at], rows), NN) + dot(recv_t, by_dst, NN)
        sigma = sigmoid(pre)
        slope_ref[:, at] = (sigma * (1.0 + pre * (1.0 - sigma))).astype(BF)
        acc_ref[...] += dot(by_dst, (pre * sigma).astype(BF), NT)
        return carry

    lax.fori_loop(0, src_ref.shape[1] // size, step, 0)


def edges_backward(src_ref, dst_ref, grad_t, slope_ref, by_src_ref, by_dst_ref, size):
    by_src_ref[...] = jnp.zeros_like(by_src_ref)
    by_dst_ref[...] = jnp.zeros_like(by_dst_ref)

    def step(i, carry):
        at = pl.ds(pl.multiple_of(i * size, size), size)
        by_dst = hot(dst_ref[:, at], by_dst_ref.shape[0])
        gpre = (dot(grad_t, by_dst, NN) * slope_ref[:, at].astype(F32)).astype(BF)
        by_src_ref[...] += dot(hot(src_ref[:, at], by_src_ref.shape[0]), gpre, NT)
        by_dst_ref[...] += dot(by_dst, gpre, NT)
        return carry

    lax.fori_loop(0, src_ref.shape[1] // size, step, 0)


def fine_forward_kernel(
    size, slots, coarse, src_ref, dst_ref, pool_ref, rows_ref, even_ref, got_ref, prev_ref,
    next_ref, cot_ref, send_ref, recv_ref, node_ref, *refs,
):
    chips = even_ref.shape[0] // slots
    landed = refs[: chips - 1]
    (upd_ref, mine_ref, other_ref, slope_ref, ext_ref, src_row_ref, pool_row_ref,
     acc_ref) = refs[chips - 1 :]
    me = lax.axis_index("dom")
    count, width = cot_ref.shape
    halo = 2 * chips * slots
    rim = prev_ref.shape[0]
    ext_ref[:count, :] = rows_ref[...]
    ext_ref[count : count + slots, :] = even_ref[:slots, :]
    ext_ref[count + slots : count + 2 * slots, :] = got_ref[:slots, :]
    for chip, ref in enumerate(landed, 1):
        at = count + 2 * chip * slots
        ext_ref[at : at + 2 * slots, :] = ref[: 2 * slots, :]
    ext_ref[count + halo : count + halo + rim, :] = prev_ref[...]
    ext_ref[count + halo + rim :, :] = next_ref[...]

    log2(slots)
    src = src_ref[...]
    inside = (src >= count) & (src < count + halo)
    src_row_ref[...] = jnp.where(inside, count + ((src - count) ^ (me * slots)), src)
    pool = pool_ref[...]
    bits = log2(coarse)
    pool_row = place(pool >> bits, me & 1, chips) * coarse + (pool & (coarse - 1))
    pool_row_ref[...] = pool_row

    own = rows_ref[...]
    send_t = dot(send_ref[...].T, ext_ref[...], NT).astype(BF)
    recv_t = dot(recv_ref[...].T, own, NT).astype(BF)
    edges_forward(src_row_ref, dst_ref, send_t, recv_t, slope_ref, acc_ref, size)
    updated = (own.astype(F32) + dot(acc_ref[...].astype(BF), node_ref[...], NN)).astype(BF)
    upd_ref[...] = updated
    both = jnp.concatenate([updated, cot_ref[...]], axis=1)
    half = mine_ref.shape[0]
    part = dot(hot(pool_row, 2 * half), both, NN).astype(BF)
    mine_ref[...] = part[:half]
    other_ref[...] = part[half:]


def add_kernel(out_ref_first, *refs):
    *parts, out_ref = (out_ref_first,) + refs
    out_ref[...] = tree_sum([part[...] for part in parts]).astype(out_ref.dtype)


def coarse_forward_kernel(
    pay, size, coarse, mine_ref, other_ref, send_ref, recv_ref, node_ref, pay_ref, got_ref, *refs
):
    (*landed, message_ref, mid_ref, slope_ref, src_ref, dst_ref, ext_ref, pool_ref, acc_ref,
     sends_ref, highs_ref, lows_ref) = refs
    me = lax.axis_index("dom")
    core = me & 1
    rows = pay.rows
    chips = len(landed) + 1
    doms = 2 * chips
    half, both_width = mine_ref.shape
    width = both_width // 2
    group_coarse = 2 * half
    skip = got_ref.shape[0] - rows
    slots2 = landed[0].shape[0] - 2 * rows
    payloads = [pay_ref[...], got_ref[skip:, :]]
    for ref in landed:
        payloads += [ref[slots2 : slots2 + rows, :], ref[slots2 + rows :, :]]
    payloads = [payload.astype(F32) for payload in payloads]

    cedges = pay.edges * 128
    cslots_all = ext_ref.shape[1] // doms
    for j, payload in enumerate(payloads):
        spot = place(me ^ j, core, chips) * coarse
        for line in range(pay.edges):
            here = slice(j * cedges + line * 128, j * cedges + line * 128 + 128)
            src = payload[line : line + 1, :].astype(jnp.int32)
            away = group_coarse + j * cslots_all - coarse
            src_ref[:, here] = src + jnp.where(src < coarse, spot, away)
            dst = payload[pay.dst + line : pay.dst + line + 1, :].astype(jnp.int32)
            dst_ref[:, here] = dst + spot
    total = tree_sum(payloads)
    sends_ref[...] = total[pay.send : pay.send + doms, :]
    owner = lanes(128) >> log2(cslots_all // doms)
    spots = place(owner, core, chips) * coarse
    per_line = 128 // cslots_all
    for line in range(doms // per_line):
        joined = jnp.full((1, 128), -1, jnp.int32)
        for part in range(per_line):
            dom = me ^ (line * per_line + part)
            row = sends_ref[pl.ds(dom, 1), :].astype(jnp.int32)
            row = jnp.where(row < coarse, row + spots, -1)
            if part:
                row = pltpu.roll(row, part * cslots_all, 1)
            joined = jnp.where(lanes(128) // cslots_all == part, row, joined)
        ext_ref[:, line * 128 : line * 128 + 128] = joined
    highs_ref[...] = total[pay.high : pay.high + pay.lines, :]
    lows_ref[...] = total[pay.low : pay.low + pay.lines, :]
    upper = pay.lines // 2
    message_ref[half:, :] = jnp.zeros_like(message_ref[half:, :])
    high_rows, low_rows = [], []
    for line in range(pay.lines):
        at = pl.ds((line + core * upper) & (pay.lines - 1), 1)
        high, low = highs_ref[at, :], lows_ref[at, :]
        pool_ref[:, line * 128 : line * 128 + 128] = (high * 128.0 + low).astype(jnp.int32)
        if line < upper:
            high_rows.append(high)
            low_rows.append(low)
    tail = message_ref.shape[0] - half - upper
    zeros = [jnp.zeros((tail, 128), F32)]
    ids = jnp.concatenate(
        [jnp.concatenate(high_rows + zeros, axis=0), jnp.concatenate(low_rows + zeros, axis=0)],
        axis=1,
    )
    message_ref[half:, :] = ids.astype(BF)

    mid_ref[:half, :] = mine_ref[...]
    mid_ref[half:, :] = other_ref[...]
    own = (0.25 * mid_ref[:, :width].astype(F32)).astype(BF)
    send_t = dot(send_ref[...].T, own, NT).astype(BF)
    recv_t = dot(recv_ref[...].T, own, NT).astype(BF)
    away = dot(send_t, hot(ext_ref[...], group_coarse), NN).astype(BF)
    send_t = jnp.concatenate([send_t, away], axis=1)
    edges_forward(src_ref, dst_ref, send_t, recv_t, slope_ref, acc_ref, size)
    mid = (own.astype(F32) + dot(acc_ref[...].astype(BF), node_ref[...], NN)).astype(BF)
    mid_ref[:, :width] = mid
    message_ref[:half, :width] = mid[:half]
    message_ref[:half, width:] = mine_ref[:, width:]


def coarse_backward_kernel(
    size, src_ref, dst_ref, ext_ref, pool_ref, mid_ref, slope_ref, top_ref, send_ref, recv_ref,
    node_ref, *refs,
):
    *others, out_ref, by_src_ref, by_dst_ref, mids_ref = refs
    own_count, width = by_dst_ref.shape
    half = own_count // 2
    mids_ref[:own_count, :] = mid_ref[...]
    rows = [pool_ref[...]]
    for i, ref in enumerate(others):
        mids_ref[own_count + i * half : own_count + i * half + half, :] = ref[:half, :]
        ids = ref[half:, :].astype(F32)
        for line in range(half // 128):
            high, low = ids[line : line + 1, :128], ids[line : line + 1, 128:]
            rows.append((high * 128.0 + low).astype(jnp.int32))
    mids = mids_ref[...]
    own = mid_ref[...].astype(F32)
    pools = hot(jnp.concatenate(rows, axis=1), NCC)
    sums = dot(pools, mids, NN)
    pooled = 0.125 * sums[:, :width]
    grad_top = sums[:, width:]
    weight = top_ref[...]
    slope_in = dot(pooled.astype(BF), weight, NN)
    sigma = sigmoid(slope_in)
    top_out = (pooled + slope_in * sigma).astype(BF)
    inner = (grad_top * (sigma * (1.0 + slope_in * (1.0 - sigma)))).astype(BF)
    grad_pool = 0.125 * (grad_top + dot(inner, weight, NT))
    both = jnp.concatenate([top_out, grad_pool.astype(BF)], axis=1)
    at_node = dot(pools[:, :own_count], both, TN)
    coarse_out = (own[:, :width] + at_node[:, :width]).astype(BF)
    grad = own[:, width:] + at_node[:, width:]
    grad_t = dot(node_ref[...], grad.astype(BF), NT).astype(BF)
    edges_backward(src_ref, dst_ref, grad_t, slope_ref, by_src_ref, by_dst_ref, size)
    by_src = by_src_ref[...]
    away = dot(hot(ext_ref[...], own_count), by_src[own_count:].astype(BF), NN)
    grad = grad + dot((by_src[:own_count] + away).astype(BF), send_ref[...], NT)
    grad = grad + dot(by_dst_ref[...].astype(BF), recv_ref[...], NT)
    out_ref[...] = jnp.concatenate([coarse_out, (0.25 * grad).astype(BF)], axis=1)


def fine_backward_kernel(
    size, slots, src_ref, dst_ref, pool_ref, ext_ref, cot_ref, upd_ref, coarse_ref, slope_ref,
    send_ref, recv_ref, node_ref, flow_ref, own_ref, odd_ref, even_ref, weight_ref, prev_ref,
    next_ref, by_src_ref, by_dst_ref, all_ref,
):
    core = lax.axis_index("dom") & 1
    count, width = cot_ref.shape
    at_node = dot(hot(pool_ref[...], coarse_ref.shape[0]), coarse_ref[...], TN)
    flow_ref[...] = (upd_ref[...].astype(F32) + at_node[:, :width]).astype(BF)
    grad = cot_ref[...].astype(F32) + at_node[:, width:]
    own_ref[...] = grad
    grad_t = dot(node_ref[...], grad.astype(BF), NT).astype(BF)
    edges_backward(src_ref, dst_ref, grad_t, slope_ref, by_src_ref, by_dst_ref, size)
    by_src = by_src_ref[...].astype(BF)
    grad_ext = dot(by_src, send_ref[...], NT)
    away = grad_ext[count:].astype(BF)
    pairs = even_ref.shape[0] // slots
    for chip in range(pairs):
        at = 2 * chip * slots
        even_ref[chip * slots : chip * slots + slots, :] = away[at : at + slots]
        odd_ref[chip * slots : chip * slots + slots, :] = away[at + slots : at + 2 * slots]
    halo = 2 * pairs * slots
    rim = prev_ref.shape[0]
    prev_ref[...] = away[halo : halo + rim]
    next_ref[...] = away[halo + rim :]
    own_ref[...] += grad_ext[:count] + dot(by_dst_ref[...].astype(BF), recv_ref[...], NT)
    all_ref[...] = dot(ext_ref[...], by_src, TN)
    half = width // 2
    weight_ref[...] = all_ref[pl.ds(pl.multiple_of(core * half, half), half), :].astype(BF)
    there = pl.ds(pl.multiple_of((1 - core) * half, half), half)
    odd_ref[pairs * slots :, :] = all_ref[there, :].astype(BF)


def pack_back_kernel(slots, even_ref, got_ref, weight_ref, *refs):
    *out_refs, half_ref = refs
    chips = len(out_refs) + 1
    half = weight_ref[...].astype(F32) + got_ref[chips * slots :, :].astype(F32)
    half_ref[...] = half.astype(BF)
    for chip, ref in enumerate(out_refs, 1):
        ref[:slots, :] = even_ref[chip * slots : chip * slots + slots, :]
        ref[slots : 2 * slots, :] = got_ref[chip * slots : chip * slots + slots, :]
        ref[2 * slots :, :] = half.astype(BF)


def weight_kernel(skip, half_ref, *refs):
    *landed, out_ref = refs
    parts = [half_ref[...]] + [ref[skip:, :] for ref in landed]
    out_ref[...] = tree_sum(parts).astype(BF)


def return_kernel(
    send_ref, rim_ref, own_ref, even_ref, got_ref, first_ref, second_ref, *refs
):
    *landed, out_ref, rows_ref = refs
    me = lax.axis_index("dom")
    doms, slots = send_ref.shape
    pieces = [even_ref[:slots, :], got_ref[:slots, :]]
    for ref in landed:
        pieces += [ref[:slots, :], ref[slots : 2 * slots, :]]
    for j, piece in enumerate(pieces):
        rows_ref[pl.ds(pl.multiple_of((me ^ j) * slots, slots), slots), :] = piece
    count = own_ref.shape[0]
    total = own_ref[...] + dot(hot(send_row(send_ref), count), rows_ref[...], NN)
    total = total + dot(hot(rim_ref[0:1, :], count), first_ref[...], NN)
    out_ref[...] = total + dot(hot(rim_ref[1:2, :], count), second_ref[...], NN)


def join_kernel(mine_ref, other_ref, out_ref):
    core = lax.axis_index("dom") & 1
    half = mine_ref.shape[0]
    out_ref[pl.ds(pl.multiple_of(core * half, half), half), :] = mine_ref[...]
    out_ref[pl.ds(pl.multiple_of((1 - core) * half, half), half), :] = other_ref[...]


def to_xor(value, axis, offset):
    count = lax.axis_size(axis)
    return lax.ppermute(value, axis, [(i, i ^ offset) for i in range(count)])


def local(
    features, cotangent, fine_send, fine_rim, fine_src, fine_dst, fine_pool, coarse_send,
    coarse_src, coarse_dst, coarse_pool, w_send, w_recv, w_node, v_send, v_recv, v_node, w_top,
):
    count, width = features.shape
    doms = lax.axis_size("dom")
    groups = lax.axis_size("group")
    chips = doms // 2
    slots = fine_send.shape[1]
    cslots = coarse_send.shape[1]
    rim = fine_rim.shape[1]
    coarse = coarse_pool.shape[0]
    group_coarse = coarse * doms
    half_coarse = group_coarse // 2
    edges = fine_src.shape[0]
    cedges = coarse_src.shape[0]
    forward = [(i, i + 1) for i in range(groups - 1)]
    backward = [(i + 1, i) for i in range(groups - 1)]
    ext_count = count + doms * slots + 2 * rim
    cext_count = group_coarse + doms * doms * cslots
    pay = Payload(cedges, group_coarse, doms)
    assert coarse + doms * cslots <= 256 and doms * cslots <= 128 and width == 128
    src_row = fine_src.reshape(1, -1)
    dst_row = fine_dst.reshape(1, -1)

    odd, even, payload, first, second = call(
        functools.partial(start_kernel, pay),
        [((chips * slots + pay.rows, width), BF), ((chips * slots, width), BF),
         ((pay.rows, width), BF), ((rim, width), BF), ((rim, width), BF)],
        fine_send, fine_rim, features, coarse_src.reshape(-1, 128), coarse_dst.reshape(-1, 128),
        coarse_pool.reshape(1, -1), coarse_send,
        scratch=[((doms * slots, width), BF), ((pay.rows, 128), F32)],
    )
    got = to_xor(odd, "dom", 1)
    messages = call(
        functools.partial(pack_kernel, slots),
        [((2 * slots + 2 * pay.rows, width), BF)] * (chips - 1), even, got, payload,
    )
    landed = [to_xor(message, "dom", 2 * o) for o, message in enumerate(messages, 1)]
    from_next = lax.ppermute(first, "group", backward)
    from_prev = lax.ppermute(second, "group", forward)

    size = chunk_of(edges, 1024)
    updated, mine, other, slope, extended, src_row, pool_row = call(
        functools.partial(fine_forward_kernel, size, slots, coarse),
        [((count, width), BF), ((half_coarse, 2 * width), BF), ((half_coarse, 2 * width), BF),
         ((width, edges), BF), ((ext_count, width), BF), ((1, edges), jnp.int32),
         ((1, count), jnp.int32)],
        src_row, dst_row, fine_pool.reshape(1, -1), features, even, got, from_prev, from_next,
        cotangent, w_send, w_recv, w_node, *landed,
        scratch=[((count, width), F32)],
    )
    half_sum = [((half_coarse, 2 * width), BF)]
    (mine,) = call(add_kernel, half_sum, mine, to_xor(other, "dom", 1))
    parts = [to_xor(mine, "dom", 2 * o) for o in range(1, chips)]
    (mine,) = call(add_kernel, half_sum, mine, *parts)
    other = to_xor(mine, "dom", 1)

    csize = chunk_of(cedges * doms, 512)
    extra = 3 * cext_count * 2 * max(csize, group_coarse)
    tail = -(-(pay.lines // 2) // 16) * 16
    message, mid, cslope, csrc_row, cdst_row, cext_row, pools = call(
        functools.partial(coarse_forward_kernel, pay, csize, coarse),
        [((half_coarse + tail, 2 * width), BF), ((group_coarse, 2 * width), BF),
         ((width, cedges * doms), BF), ((1, cedges * doms), jnp.int32),
         ((1, cedges * doms), jnp.int32), ((1, doms * doms * cslots), jnp.int32),
         ((1, group_coarse), jnp.int32)],
        mine, other, v_send, v_recv, v_node, payload, got, *landed,
        scratch=[((group_coarse, width), F32), ((doms, 128), F32), ((pay.lines, 128), F32),
                 ((pay.lines, 128), F32)],
        extra=extra,
    )
    others = [to_xor(message, "group", o) for o in range(1, groups)]
    others += [to_xor(part, "dom", 1) for part in others]
    (back,) = call(
        functools.partial(coarse_backward_kernel, csize),
        [((group_coarse, 2 * width), BF)],
        csrc_row, cdst_row, cext_row, pools, mid, cslope, w_top, v_send, v_recv, v_node, *others,
        scratch=[((cext_count, width), F32), ((group_coarse, width), F32),
                 ((groups * group_coarse, 2 * width), BF)],
        extra=extra,
    )

    half = width // 2
    flow, own, odd, even, weight, prev_grad, next_grad = call(
        functools.partial(fine_backward_kernel, size, slots),
        [((count, width), BF), ((count, width), F32), ((chips * slots + half, width), BF),
         ((chips * slots, width), BF), ((half, width), BF), ((rim, width), BF),
         ((rim, width), BF)],
        src_row, dst_row, pool_row, extended, cotangent, updated, back, slope, w_send, w_recv,
        w_node,
        scratch=[((ext_count, width), F32), ((count, width), F32), ((width, width), F32)],
    )

    got = to_xor(odd, "dom", 1)
    *messages, weight = call(
        functools.partial(pack_back_kernel, slots),
        [((2 * slots + half, width), BF)] * (chips - 1) + [((half, width), BF)],
        even, got, weight,
    )
    landed = [to_xor(message, "dom", 2 * o) for o, message in enumerate(messages, 1)]
    to_first = lax.ppermute(next_grad, "group", forward)
    to_second = lax.ppermute(prev_grad, "group", backward)
    (weight,) = call(
        functools.partial(weight_kernel, 2 * slots), [((half, width), BF)], weight, *landed
    )
    parts = [to_xor(weight, "group", o) for o in range(1, groups)]
    (grad_x,) = call(
        return_kernel, [((count, width), F32)],
        fine_send, fine_rim, own, even, got, to_first, to_second, *landed,
        scratch=[((doms * slots, width), BF)],
    )
    (weight,) = call(add_kernel, [((half, width), F32)], weight, *parts)
    (grad_send,) = call(
        join_kernel, [((width, width), F32)], weight, to_xor(weight, "dom", 1)
    )
    return flow, grad_x, grad_send


def solution(mesh):
    rows = P(("group", "dom"), None)
    line = P(("group", "dom"))
    placed = (rows, rows, rows, rows, line, line, line, rows, line, line, line) + (P(),) * 7
    return jax.shard_map(
        local, mesh=mesh, in_specs=placed, out_specs=(rows, rows, P()), check_vma=False
    )
```

time: 104 us -> 84 us (0.81)
  Pallas kernels: 29.5 us -> 20.6 us
  waiting for transfers between devices: 17.2 us -> 24.7 us
  local copies, waits for them, and re-layouts: 13 us -> 6.18 us
  starting transfers between devices: 37.4 us -> 31.2 us
  other arithmetic: 5.14 us -> 0 us
    pallas_call x6 -> x13, Pallas kernels: 29.5 us -> 20.6 us  [call(): pl.pallas_call(kernel, out_shape=[jax.ShapeDtypeStruct(shape, kind) for s...]
    ppermute x4, waiting for transfers between devices: 0.01 us -> 5.3 us  [the longest x1 4.23 us: local(): to_second = lax.ppermute(prev_grad, 'group', backward)]
    all_to_all x1 -> x0, starting transfers between devices: 5.2 us -> none  [local(): lax.all_to_all(jnp.broadcast_to(table[None], (doms, table.shape[0])), 'do...]
    slice x10 -> x0, local copies, waits for them, and re-layouts: 3.57 us -> none  [the longest x1 0.92 us: local(): got = to_xor(part[half_coarse:], 'dom', 1)]
    concatenate x13 -> x0, other arithmetic: 3.55 us -> none  [the longest x1 0.82 us: local(): jnp.concatenate([mid, others[:, :, :half_coarse].reshape(-1, 2 * width)],...]
    ppermute x4, starting transfers between devices: 11.7 us -> 9.08 us  [the longest x1 4.49 us: local(): from_prev = lax.ppermute(second, 'group', forward)]
    ppermute x21 -> x23, waiting for transfers between devices: 17.2 us -> 19.4 us  [to_xor(): return lax.ppermute(value, axis, [(i, i ^ offset) for i in range(count)])]
    ppermute x21 -> x23, starting transfers between devices: 20.5 us -> 22.1 us  [to_xor(): return lax.ppermute(value, axis, [(i, i ^ offset) for i in range(count)])]
  transfers between devices with their start and end apart: 26 -> 27, of which waited for: 13 -> 17; matrix products, arithmetic and copies ran while one was open for 5% -> 0% of each run, Pallas kernels for 4% -> 1%
where the time goes in v2:
time: 84 us; the launch traced here: 83.5 us
  starting transfers between devices  31.2 us (37%)
  waiting for transfers between devices  24.7 us (29%)
  Pallas kernels  20.6 us (25%)
  local copies, waits for them, and re-layouts  6.18 us (7%)
  between operations  0.9 us (1%)
    ppermute x23, starting transfers between devices, to_xor(): return lax.ppermute(value, axis, [(i, i ^ offset) for i in range(count)])  22.1 us
    pallas_call x13, Pallas kernels, call(): pl.pallas_call(kernel, out_shape=[jax.ShapeDtypeStruct(shape, kind) for s...  20.6 us
    ppermute x23, waiting for transfers between devices, to_xor(): return lax.ppermute(value, axis, [(i, i ^ offset) for i in range(count)])  19.4 us
    unnamed x43, local copies, waits for them, and re-layouts  6.18 us
    ppermute x1, starting transfers between devices, local(): from_prev = lax.ppermute(second, 'group', forward)  4.49 us
    ppermute x1, waiting for transfers between devices, local(): to_second = lax.ppermute(prev_grad, 'group', backward)  4.23 us
    ppermute x1, starting transfers between devices, local(): to_first = lax.ppermute(next_grad, 'group', forward)  2.01 us
  transfers between devices with their start and end apart: 27, of which 17 were waited for; matrix products, arithmetic and copies ran while one was open for 0% of the time, Pallas kernels for 1%

profile of v2, /device:TPU:0, one launch (start us, length us, event | category | flops | bytes accessed | tf_op | source)
XLA Modules:
  0.0 83.5 jit_solution(13705133647177916335)
XLA Ops:
  4.0 4.5 %collective-permute-start.1 = (bf16[128,128]{1,0:T(8,128)(2,1)S(1)}, bf16[128,128]{1,0:T(8,128)(2,1)S(1)}, u32[]{:S(2)}, u32[]{:S(2)}) collective-permute-start(bf16[128,128]{1,0:T(8,128)(2,1)S(1)} %get-tuple-element.38), channel_id=1, source_target_pairs={{0,8},{8,16},{16,24},{1,9},{9,17},{17,25},{2,10},{10,18},{18,26},{... | collective-permute-start | bytes 98312 | tf_op jit(solution)/shard_map/ppermute | solution.py:471
  8.5 1.3 %collective-permute-start.2 = (bf16[128,128]{1,0:T(8,128)(2,1)S(1)}, bf16[128,128]{1,0:T(8,128)(2,1)S(1)}, u32[]{:S(2)}, u32[]{:S(2)}) collective-permute-start(bf16[128,128]{1,0:T(8,128)(2,1)S(1)} %get-tuple-element.39), channel_id=1, source_target_pairs={{8,0},{16,8},{24,16},{9,1},{17,9},{25,17},{10,2},{18,10},{26,18},{... | collective-permute-start | bytes 98312 | tf_op jit(solution)/shard_map/ppermute | solution.py:470
  9.9 1.6 %collective-permute-start.3 = (bf16[64,128]{1,0:T(8,128)(2,1)S(1)}, bf16[64,128]{1,0:T(8,128)(2,1)S(1)}, u32[]{:S(2)}, u32[]{:S(2)}) collective-permute-start(bf16[64,128]{1,0:T(8,128)(2,1)S(1)} %get-tuple-element.41), channel_id=1, source_target_pairs={{0,2},{1,3},{2,0},{3,1},{4,6},{5,7},{6,4},{7,5},{8,10},{9,11},{10,... | collective-permute-start | bytes 49160 | tf_op jit(solution)/shard_map/ppermute | solution.py:428
  11.4 1.5 %collective-permute-start.4 = (bf16[64,128]{1,0:T(8,128)(2,1)S(1)}, bf16[64,128]{1,0:T(8,128)(2,1)S(1)}, u32[]{:S(2)}, u32[]{:S(2)}) collective-permute-start(bf16[64,128]{1,0:T(8,128)(2,1)S(1)} %get-tuple-element.42), channel_id=1, source_target_pairs={{0,4},{1,5},{2,6},{3,7},{4,0},{5,1},{6,2},{7,3},{8,12},{9,13},{10,... | collective-permute-start | bytes 49160 | tf_op jit(solution)/shard_map/ppermute | solution.py:428
  15.1 2.4 %collective-permute-done.5.refs_2_ = bf16[64,128]{1,0:T(8,128)(2,1)S(1)} collective-permute-done((bf16[64,128]{1,0:T(8,128)(2,1)S(1)}, bf16[64,128]{1,0:T(8,128)(2,1)S(1)}, u32[]{:S(2)}, u32[]{:S(2)}) %collective-permute-start.5) | collective-permute-done | bytes 16416 | tf_op jit(solution)/shard_map/ppermute | solution.py:428
  21.4 5.2 %shard_map.195 = (bf16[512,128]{1,0:T(8,128)(2,1)S(1)}, bf16[128,256]{1,0:T(8,128)(2,1)S(1)}, bf16[128,256]{1,0:T(8,128)(2,1)S(1)}, bf16[128,4096]{1,0:T(8,128)(...) custom-call(s32[1,4096]{1,0:T(1,128)S(1)} %bitcast.8, s32[1,4096]{1,0:T(1,128)S(1)} %bitcast.6, ...), custom_call_target="tpu_custom_call" | custom-call | tf_op jit(solution)/shard_map/pallas_call | solution.py:43
  28.5 1.5 %collective-permute-start.8 = (bf16[128,256]{1,0:T(8,128)(2,1)S(1)}, bf16[128,256]{1,0:T(8,128)(2,1)S(1)}, u32[]{:S(2)}, u32[]{:S(2)}) collective-permute-start(bf16[128,256]{1,0:T(8,128)(2,1)S(1)} %shard_map.196.out_ref_first), channel_id=1, source_target_pairs={{0,4},{1,5},{2,6},{3,7},{4,0},{5,1},{6,2},{7,3},{8,12},{9,13},{10,... | collective-permute-start | bytes 196616 | tf_op jit(solution)/shard_map/ppermute | solution.py:428
  30.0 1.5 %collective-permute-start.7 = (bf16[128,256]{1,0:T(8,128)(2,1)S(1)}, bf16[128,256]{1,0:T(8,128)(2,1)S(1)}, u32[]{:S(2)}, u32[]{:S(2)}) collective-permute-start(bf16[128,256]{1,0:T(8,128)(2,1)S(1)} %shard_map.196.out_ref_first), channel_id=1, source_target_pairs={{0,2},{1,3},{2,0},{3,1},{4,6},{5,7},{6,4},{7,5},{8,10},{9,11},{10,... | collective-permute-start | bytes 196616 | tf_op jit(solution)/shard_map/ppermute | solution.py:428
  31.5 2.3 %collective-permute-done.9.refs_2_ = bf16[128,256]{1,0:T(8,128)(2,1)S(1)} collective-permute-done((bf16[128,256]{1,0:T(8,128)(2,1)S(1)}, bf16[128,256]{1,0:T(8,128)(2,1)S(1)}, u32[]{:S(2)}, u32[]{:S(2)}) %collective-permute-start.9) | collective-permute-done | bytes 65568 | tf_op jit(solution)/shard_map/ppermute | solution.py:428
  35.6 2.8 %shard_map.198 = (bf16[144,256]{1,0:T(8,128)(2,1)S(1)}, bf16[256,256]{1,0:T(8,128)(2,1)S(1)}, bf16[128,2048]{1,0:T(8,128)(2,1)S(1)}, s32[1,2048]{1,0:T(1,128)S(1...) custom-call(bf16[128,256]{1,0:T(8,128)(2,1)S(1)} %shard_map.197.mine_ref, ...), custom_call_target="tpu_custom_call" | custom-call | tf_op jit(solution)/shard_map/pallas_call | solution.py:43
  38.4 4.7 %collective-permute-start.13 = (bf16[144,256]{1,0:T(8,128)(2,1)S(1)}, bf16[144,256]{1,0:T(8,128)(2,1)S(1)}, u32[]{:S(2)}, u32[]{:S(2)}) collective-permute-start(bf16[144,256]{1,0:T(8,128)(2,1)S(1)} %get-tuple-element.56), channel_id=1, source_target_pairs={{0,24},{8,16},{16,8},{24,0},{1,25},{9,17},{17,9},{25,1},{2,26},{10... | collective-permute-start | bytes 221192 | tf_op jit(solution)/shard_map/ppermute | solution.py:428
  43.8 2.3 %collective-permute-done.13.refs_2_ = bf16[144,256]{1,0:T(8,128)(2,1)S(1)} collective-permute-done((bf16[144,256]{1,0:T(8,128)(2,1)S(1)}, bf16[144,256]{1,0:T(8,128)(2,1)S(1)}, u32[]{:S(2)}, u32[]{:S(2)}) %collective-permute-start.13) | collective-permute-done | bytes 73760 | tf_op jit(solution)/shard_map/ppermute | solution.py:428
  46.1 3.6 %collective-permute-done.12.refs_1_ = bf16[144,256]{1,0:T(8,128)(2,1)S(1)} collective-permute-done((bf16[144,256]{1,0:T(8,128)(2,1)S(1)}, bf16[144,256]{1,0:T(8,128)(2,1)S(1)}, u32[]{:S(2)}, u32[]{:S(2)}) %collective-permute-start.12) | collective-permute-done | bytes 73760 | tf_op jit(solution)/shard_map/ppermute | solution.py:428
  51.1 3.9 %shard_map.199.coarse_ref = bf16[256,256]{1,0:T(8,128)(2,1)S(1)} custom-call(s32[1,2048]{1,0:T(1,128)S(1)} %get-tuple-element.50.src_ref, s32[1,2048]{1,0:T(1,128)S(1)} %get-tuple-element.51.dst_ref, s32[1,256]{1,0:T(1,128)S(1)} %get-tuple-element.52.ext_ref, s32[1,256]{1,0:T(1,128)S(1)} %get-tuple-element.53.pool_ref, ...), custom_call_target="tpu_custom_call" | custom-call | tf_op jit(solution)/shard_map/pallas_call | solution.py:43
  55.0 6.5 %shard_map.200 = (bf16[512,128]{1,0:T(8,128)(2,1)}, f32[512,128]{1,0:T(8,128)S(1)}, bf16[128,128]{1,0:T(8,128)(2,1)S(1)}, bf16[64,128]{1,0:T(8,128)(2,1)S(1)}, b...) custom-call(s32[1,4096]{1,0:T(1,128)S(1)} %get-tuple-element.44.src_ref, ...), custom_call_target="tpu_custom_call" | custom-call | tf_op jit(solution)/shard_map/pallas_call | solution.py:43
  62.7 1.6 %collective-permute-start.20 = (bf16[96,128]{1,0:T(8,128)(2,1)S(1)}, bf16[96,128]{1,0:T(8,128)(2,1)S(1)}, u32[]{:S(2)}, u32[]{:S(2)}) collective-permute-start(bf16[96,128]{1,0:T(8,128)(2,1)S(1)} %get-tuple-element.65), channel_id=1, source_target_pairs={{0,2},{1,3},{2,0},{3,1},{4,6},{5,7},{6,4},{7,5},{8,10},{9,11},{10,... | collective-permute-start | bytes 73736 | tf_op jit(solution)/shard_map/ppermute | solution.py:428
  64.8 1.5 %collective-permute-start.22 = (bf16[96,128]{1,0:T(8,128)(2,1)S(1)}, bf16[96,128]{1,0:T(8,128)(2,1)S(1)}, u32[]{:S(2)}, u32[]{:S(2)}) collective-permute-start(bf16[96,128]{1,0:T(8,128)(2,1)S(1)} %get-tuple-element.67), channel_id=1, source_target_pairs={{0,6},{1,7},{2,4},{3,5},{4,2},{5,3},{6,0},{7,1},{8,14},{9,15},{10,... | collective-permute-start | bytes 73736 | tf_op jit(solution)/shard_map/ppermute | solution.py:428
  66.6 1.5 %collective-permute-done.21.refs_1_ = bf16[96,128]{1,0:T(8,128)(2,1)S(1)} collective-permute-done((bf16[96,128]{1,0:T(8,128)(2,1)S(1)}, bf16[96,128]{1,0:T(8,128)(2,1)S(1)}, u32[]{:S(2)}, u32[]{:S(2)}) %collective-permute-start.21) | collective-permute-done | bytes 24608 | tf_op jit(solution)/shard_map/ppermute | solution.py:428
  68.1 1.4 %collective-permute-done.22.refs_2_ = bf16[96,128]{1,0:T(8,128)(2,1)S(1)} collective-permute-done((bf16[96,128]{1,0:T(8,128)(2,1)S(1)}, bf16[96,128]{1,0:T(8,128)(2,1)S(1)}, u32[]{:S(2)}, u32[]{:S(2)}) %collective-permute-start.22) | collective-permute-done | bytes 24608 | tf_op jit(solution)/shard_map/ppermute | solution.py:428
  69.5 2.5 %collective-permute-start.25 = (bf16[64,128]{1,0:T(8,128)(2,1)S(1)}, bf16[64,128]{1,0:T(8,128)(2,1)S(1)}, u32[]{:S(2)}, u32[]{:S(2)}) collective-permute-start(bf16[64,128]{1,0:T(8,128)(2,1)S(1)} %shard_map.203.out_ref_first), channel_id=1, source_target_pairs={{0,24},{8,16},{16,8},{24,0},{1,25},{9,17},{17,9},{25,1},{2,26},{10... | collective-permute-start | bytes 49160 | tf_op jit(solution)/shard_map/ppermute | solution.py:428
  72.1 1.9 %collective-permute-start.23 = (bf16[64,128]{1,0:T(8,128)(2,1)S(1)}, bf16[64,128]{1,0:T(8,128)(2,1)S(1)}, u32[]{:S(2)}, u32[]{:S(2)}) collective-permute-start(bf16[64,128]{1,0:T(8,128)(2,1)S(1)} %shard_map.203.out_ref_first), channel_id=1, source_target_pairs={{0,8},{8,0},{16,24},{24,16},{1,9},{9,1},{17,25},{25,17},{2,10},{10... | collective-permute-start | bytes 49160 | tf_op jit(solution)/shard_map/ppermute | solution.py:428
  74.0 2.0 %collective-permute-start.18 = (bf16[128,128]{1,0:T(8,128)(2,1)S(1)}, bf16[128,128]{1,0:T(8,128)(2,1)S(1)}, u32[]{:S(2)}, u32[]{:S(2)}) collective-permute-start(bf16[128,128]{1,0:T(8,128)(2,1)S(1)} %get-tuple-element.62), channel_id=1, source_target_pairs={{0,8},{8,16},{16,24},{1,9},{9,17},{17,25},{2,10},{10,18},{18,26},{... | collective-permute-start | bytes 98312 | tf_op jit(solution)/shard_map/ppermute | solution.py:532
  76.0 1.3 %collective-permute-start.19 = (bf16[128,128]{1,0:T(8,128)(2,1)S(1)}, bf16[128,128]{1,0:T(8,128)(2,1)S(1)}, u32[]{:S(2)}, u32[]{:S(2)}) collective-permute-start(bf16[128,128]{1,0:T(8,128)(2,1)S(1)} %get-tuple-element.63), channel_id=1, source_target_pairs={{8,0},{16,8},{24,16},{9,1},{17,9},{25,17},{10,2},{18,10},{26,18},{... | collective-permute-start | bytes 98312 | tf_op jit(solution)/shard_map/ppermute | solution.py:533
  77.6 4.2 %collective-permute-done.19.second_ref = bf16[128,128]{1,0:T(8,128)(2,1)S(1)} collective-permute-done((bf16[128,128]{1,0:T(8,128)(2,1)S(1)}, bf16[128,128]{1,0:T(8,128)(2,1)S(1)}, u32[]{:S(2)}, u32[]{:S(2)}) %collective-permute-start.19) | collective-permute-done | bytes 32800 | tf_op jit(solution)/shard_map/ppermute | solution.py:533
  (86 shorter events, 19.2 us)
Async XLA Ops:
  3.5 6.4 %collective-permute-start = (bf16[80,128]{1,0:T(8,128)(2,1)S(1)}, bf16[80,128]{1,0:T(8,128)(2,1)S(1)}, u32[]{:S(2)}, u32[]{:S(2)}) collective-permute-start(bf16[80,128]{1,0:T(8,128)(2,1)S(1)} %get-tuple-element.37), channel_id=1, source_target_pairs={{0,1},{1,0},{2,3},{3,2},{4,5},{5,4},{6,7},{7,6},{8,9},{9,8},{10,11... | collective-permute-start | bytes 61448 | tf_op jit(solution)/shard_map/ppermute | solution.py:428
  4.0 9.4 %collective-permute-start.1 = (bf16[128,128]{1,0:T(8,128)(2,1)S(1)}, bf16[128,128]{1,0:T(8,128)(2,1)S(1)}, u32[]{:S(2)}, u32[]{:S(2)}) collective-permute-start(bf16[128,128]{1,0:T(8,128)(2,1)S(1)} %get-tuple-element.38), channel_id=1, source_target_pairs={{0,8},{8,16},{16,24},{1,9},{9,17},{17,25},{2,10},{10,18},{18,26},{... | collective-permute-start | bytes 98312 | tf_op jit(solution)/shard_map/ppermute | solution.py:471
  8.5 5.8 %collective-permute-start.2 = (bf16[128,128]{1,0:T(8,128)(2,1)S(1)}, bf16[128,128]{1,0:T(8,128)(2,1)S(1)}, u32[]{:S(2)}, u32[]{:S(2)}) collective-permute-start(bf16[128,128]{1,0:T(8,128)(2,1)S(1)} %get-tuple-element.39), channel_id=1, source_target_pairs={{8,0},{16,8},{24,16},{9,1},{17,9},{25,17},{10,2},{18,10},{26,18},{... | collective-permute-start | bytes 98312 | tf_op jit(solution)/shard_map/ppermute | solution.py:470
  9.9 4.5 %collective-permute-start.3 = (bf16[64,128]{1,0:T(8,128)(2,1)S(1)}, bf16[64,128]{1,0:T(8,128)(2,1)S(1)}, u32[]{:S(2)}, u32[]{:S(2)}) collective-permute-start(bf16[64,128]{1,0:T(8,128)(2,1)S(1)} %get-tuple-element.41), channel_id=1, source_target_pairs={{0,2},{1,3},{2,0},{3,1},{4,6},{5,7},{6,4},{7,5},{8,10},{9,11},{10,... | collective-permute-start | bytes 49160 | tf_op jit(solution)/shard_map/ppermute | solution.py:428
  11.4 3.7 %collective-permute-start.4 = (bf16[64,128]{1,0:T(8,128)(2,1)S(1)}, bf16[64,128]{1,0:T(8,128)(2,1)S(1)}, u32[]{:S(2)}, u32[]{:S(2)}) collective-permute-start(bf16[64,128]{1,0:T(8,128)(2,1)S(1)} %get-tuple-element.42), channel_id=1, source_target_pairs={{0,4},{1,5},{2,6},{3,7},{4,0},{5,1},{6,2},{7,3},{8,12},{9,13},{10,... | collective-permute-start | bytes 49160 | tf_op jit(solution)/shard_map/ppermute | solution.py:428
  12.9 4.6 %collective-permute-start.5 = (bf16[64,128]{1,0:T(8,128)(2,1)S(1)}, bf16[64,128]{1,0:T(8,128)(2,1)S(1)}, u32[]{:S(2)}, u32[]{:S(2)}) collective-permute-start(bf16[64,128]{1,0:T(8,128)(2,1)S(1)} %get-tuple-element.43), channel_id=1, source_target_pairs={{0,6},{1,7},{2,4},{3,5},{4,2},{5,3},{6,0},{7,1},{8,14},{9,15},{10,... | collective-permute-start | bytes 49160 | tf_op jit(solution)/shard_map/ppermute | solution.py:428
  26.5 1.3 %collective-permute-start.6 = (bf16[128,256]{1,0:T(8,128)(2,1)S(1)}, bf16[128,256]{1,0:T(8,128)(2,1)S(1)}, u32[]{:S(2)}, u32[]{:S(2)}) collective-permute-start(bf16[128,256]{1,0:T(8,128)(2,1)S(1)} %get-tuple-element.49), channel_id=1, source_target_pairs={{0,1},{1,0},{2,3},{3,2},{4,5},{5,4},{6,7},{7,6},{8,9},{9,8},{10,11... | collective-permute-start | bytes 196616 | tf_op jit(solution)/shard_map/ppermute | solution.py:428
  27.9 5.8 %collective-permute-start.9 = (bf16[128,256]{1,0:T(8,128)(2,1)S(1)}, bf16[128,256]{1,0:T(8,128)(2,1)S(1)}, u32[]{:S(2)}, u32[]{:S(2)}) collective-permute-start(bf16[128,256]{1,0:T(8,128)(2,1)S(1)} %shard_map.196.out_ref_first), channel_id=1, source_target_pairs={{0,6},{1,7},{2,4},{3,5},{4,2},{5,3},{6,0},{7,1},{8,14},{9,15},{10,... | collective-permute-start | bytes 196616 | tf_op jit(solution)/shard_map/ppermute | solution.py:428
  28.5 5.3 %collective-permute-start.8 = (bf16[128,256]{1,0:T(8,128)(2,1)S(1)}, bf16[128,256]{1,0:T(8,128)(2,1)S(1)}, u32[]{:S(2)}, u32[]{:S(2)}) collective-permute-start(bf16[128,256]{1,0:T(8,128)(2,1)S(1)} %shard_map.196.out_ref_first), channel_id=1, source_target_pairs={{0,4},{1,5},{2,6},{3,7},{4,0},{5,1},{6,2},{7,3},{8,12},{9,13},{10,... | collective-permute-start | bytes 196616 | tf_op jit(solution)/shard_map/ppermute | solution.py:428
  30.0 4.3 %collective-permute-start.7 = (bf16[128,256]{1,0:T(8,128)(2,1)S(1)}, bf16[128,256]{1,0:T(8,128)(2,1)S(1)}, u32[]{:S(2)}, u32[]{:S(2)}) collective-permute-start(bf16[128,256]{1,0:T(8,128)(2,1)S(1)} %shard_map.196.out_ref_first), channel_id=1, source_target_pairs={{0,2},{1,3},{2,0},{3,1},{4,6},{5,7},{6,4},{7,5},{8,10},{9,11},{10,... | collective-permute-start | bytes 196616 | tf_op jit(solution)/shard_map/ppermute | solution.py:428
  38.4 7.7 %collective-permute-start.13 = (bf16[144,256]{1,0:T(8,128)(2,1)S(1)}, bf16[144,256]{1,0:T(8,128)(2,1)S(1)}, u32[]{:S(2)}, u32[]{:S(2)}) collective-permute-start(bf16[144,256]{1,0:T(8,128)(2,1)S(1)} %get-tuple-element.56), channel_id=1, source_target_pairs={{0,24},{8,16},{16,8},{24,0},{1,25},{9,17},{17,9},{25,1},{2,26},{10... | collective-permute-start | bytes 221192 | tf_op jit(solution)/shard_map/ppermute | solution.py:428
  43.1 6.5 %collective-permute-start.12 = (bf16[144,256]{1,0:T(8,128)(2,1)S(1)}, bf16[144,256]{1,0:T(8,128)(2,1)S(1)}, u32[]{:S(2)}, u32[]{:S(2)}) collective-permute-start(bf16[144,256]{1,0:T(8,128)(2,1)S(1)} %get-tuple-element.56), channel_id=1, source_target_pairs={{0,16},{8,24},{16,0},{24,8},{1,17},{9,25},{17,1},{25,9},{2,18},{10... | collective-permute-start | bytes 221192 | tf_op jit(solution)/shard_map/ppermute | solution.py:428
  43.1 6.5 %collective-permute-start.11 = (bf16[144,256]{1,0:T(8,128)(2,1)S(1)}, bf16[144,256]{1,0:T(8,128)(2,1)S(1)}, u32[]{:S(2)}, u32[]{:S(2)}) collective-permute-start(bf16[144,256]{1,0:T(8,128)(2,1)S(1)} %get-tuple-element.56), channel_id=1, source_target_pairs={{0,8},{8,0},{16,24},{24,16},{1,9},{9,1},{17,25},{25,17},{2,10},{10... | collective-permute-start | bytes 221192 | tf_op jit(solution)/shard_map/ppermute | solution.py:428
  46.1 4.1 %collective-permute-start.16 = (bf16[144,256]{1,0:T(8,128)(2,1)S(1)}, bf16[144,256]{1,0:T(8,128)(2,1)S(1)}, u32[]{:S(2)}, u32[]{:S(2)}) collective-permute-start(bf16[144,256]{1,0:T(8,128)(2,1)S(1)} %collective-permute-done.13.refs_2_), channel_id=1, source_target_pairs={{0,1},{1,0},{2,3},{3,2},{4,5},{5,4},{6,7},{7,6},{8,9},{9,8},{10,11... | collective-permute-start | bytes 221192 | tf_op jit(solution)/shard_map/ppermute | solution.py:428
  49.7 1.4 %collective-permute-start.14 = (bf16[144,256]{1,0:T(8,128)(2,1)S(1)}, bf16[144,256]{1,0:T(8,128)(2,1)S(1)}, u32[]{:S(2)}, u32[]{:S(2)}) collective-permute-start(bf16[144,256]{1,0:T(8,128)(2,1)S(1)} %collective-permute-done.11.refs_0_), channel_id=1, source_target_pairs={{0,1},{1,0},{2,3},{3,2},{4,5},{5,4},{6,7},{7,6},{8,9},{9,8},{10,11... | collective-permute-start | bytes 221192 | tf_op jit(solution)/shard_map/ppermute | solution.py:428
  62.7 3.9 %collective-permute-start.20 = (bf16[96,128]{1,0:T(8,128)(2,1)S(1)}, bf16[96,128]{1,0:T(8,128)(2,1)S(1)}, u32[]{:S(2)}, u32[]{:S(2)}) collective-permute-start(bf16[96,128]{1,0:T(8,128)(2,1)S(1)} %get-tuple-element.65), channel_id=1, source_target_pairs={{0,2},{1,3},{2,0},{3,1},{4,6},{5,7},{6,4},{7,5},{8,10},{9,11},{10,... | collective-permute-start | bytes 73736 | tf_op jit(solution)/shard_map/ppermute | solution.py:428
  64.3 3.8 %collective-permute-start.21 = (bf16[96,128]{1,0:T(8,128)(2,1)S(1)}, bf16[96,128]{1,0:T(8,128)(2,1)S(1)}, u32[]{:S(2)}, u32[]{:S(2)}) collective-permute-start(bf16[96,128]{1,0:T(8,128)(2,1)S(1)} %get-tuple-element.66), channel_id=1, source_target_pairs={{0,4},{1,5},{2,6},{3,7},{4,0},{5,1},{6,2},{7,3},{8,12},{9,13},{10,... | collective-permute-start | bytes 73736 | tf_op jit(solution)/shard_map/ppermute | solution.py:428
  64.8 4.7 %collective-permute-start.22 = (bf16[96,128]{1,0:T(8,128)(2,1)S(1)}, bf16[96,128]{1,0:T(8,128)(2,1)S(1)}, u32[]{:S(2)}, u32[]{:S(2)}) collective-permute-start(bf16[96,128]{1,0:T(8,128)(2,1)S(1)} %get-tuple-element.67), channel_id=1, source_target_pairs={{0,6},{1,7},{2,4},{3,5},{4,2},{5,3},{6,0},{7,1},{8,14},{9,15},{10,... | collective-permute-start | bytes 73736 | tf_op jit(solution)/shard_map/ppermute | solution.py:428
  69.5 7.8 %collective-permute-start.25 = (bf16[64,128]{1,0:T(8,128)(2,1)S(1)}, bf16[64,128]{1,0:T(8,128)(2,1)S(1)}, u32[]{:S(2)}, u32[]{:S(2)}) collective-permute-start(bf16[64,128]{1,0:T(8,128)(2,1)S(1)} %shard_map.203.out_ref_first), channel_id=1, source_target_pairs={{0,24},{8,16},{16,8},{24,0},{1,25},{9,17},{17,9},{25,1},{2,26},{10... | collective-permute-start | bytes 49160 | tf_op jit(solution)/shard_map/ppermute | solution.py:428
  72.1 5.2 %collective-permute-start.24 = (bf16[64,128]{1,0:T(8,128)(2,1)S(1)}, bf16[64,128]{1,0:T(8,128)(2,1)S(1)}, u32[]{:S(2)}, u32[]{:S(2)}) collective-permute-start(bf16[64,128]{1,0:T(8,128)(2,1)S(1)} %shard_map.203.out_ref_first), channel_id=1, source_target_pairs={{0,16},{8,24},{16,0},{24,8},{1,17},{9,25},{17,1},{25,9},{2,18},{10... | collective-permute-start | bytes 49160 | tf_op jit(solution)/shard_map/ppermute | solution.py:428
  72.1 5.3 %collective-permute-start.23 = (bf16[64,128]{1,0:T(8,128)(2,1)S(1)}, bf16[64,128]{1,0:T(8,128)(2,1)S(1)}, u32[]{:S(2)}, u32[]{:S(2)}) collective-permute-start(bf16[64,128]{1,0:T(8,128)(2,1)S(1)} %shard_map.203.out_ref_first), channel_id=1, source_target_pairs={{0,8},{8,0},{16,24},{24,16},{1,9},{9,1},{17,25},{25,17},{2,10},{10... | collective-permute-start | bytes 49160 | tf_op jit(solution)/shard_map/ppermute | solution.py:428
  74.0 3.6 %collective-permute-start.18 = (bf16[128,128]{1,0:T(8,128)(2,1)S(1)}, bf16[128,128]{1,0:T(8,128)(2,1)S(1)}, u32[]{:S(2)}, u32[]{:S(2)}) collective-permute-start(bf16[128,128]{1,0:T(8,128)(2,1)S(1)} %get-tuple-element.62), channel_id=1, source_target_pairs={{0,8},{8,16},{16,24},{1,9},{9,17},{17,25},{2,10},{10,18},{18,26},{... | collective-permute-start | bytes 98312 | tf_op jit(solution)/shard_map/ppermute | solution.py:532
  76.0 5.8 %collective-permute-start.19 = (bf16[128,128]{1,0:T(8,128)(2,1)S(1)}, bf16[128,128]{1,0:T(8,128)(2,1)S(1)}, u32[]{:S(2)}, u32[]{:S(2)}) collective-permute-start(bf16[128,128]{1,0:T(8,128)(2,1)S(1)} %get-tuple-element.63), channel_id=1, source_target_pairs={{8,0},{16,8},{24,16},{9,1},{17,9},{25,17},{10,2},{18,10},{26,18},{... | collective-permute-start | bytes 98312 | tf_op jit(solution)/shard_map/ppermute | solution.py:533
  77.4 5.5 %collective-permute-start.26 = (f32[64,128]{1,0:T(8,128)S(1)}, f32[64,128]{1,0:T(8,128)S(1)}, u32[]{:S(2)}, u32[]{:S(2)}) collective-permute-start(f32[64,128]{1,0:T(8,128)S(1)} %shard_map.204.mine_ref), channel_id=1, source_target_pairs={{0,1},{1,0},{2,3},{3,2},{4,5},{5,4},{6,7},{7,6},{8,9},{9,8},{10,11... | collective-permute-start | bytes 98312 | tf_op jit(solution)/shard_map/ppermute | solution.py:428
  (24 other events, 105.7 us)
